TPU v7x, 128 devices: a whole 4x4x4 slice. The times are simulated.
128 devices in a mesh: row: 8 (over z, x_lo), col: 16 (over x_hi, y, core).
Axes of the slice: x: 4 (x_hi: 2, x_lo: 2; x = x_hi * 2 + x_lo), y: 4, z: 4, core: 2. Of those that a mesh axis runs over, the one named last changes fastest.
Arguments:
- scene_tokens: bfloat16 [128, 1024, 180], P('row', 'col'), may hold values from -8 to 8
- block_qkv: bfloat16 [3, 180, 540], replicated, may hold values from -1.8 to 1.8
- block_proj: bfloat16 [3, 180, 180], replicated, may hold values from -0.4375 to 0.4375
- conv_squeeze: bfloat16 [3, 9, 180, 60], replicated, may hold values from -0.15625 to 0.15625
- conv_expand: bfloat16 [3, 9, 60, 180], replicated, may hold values from -0.25 to 0.25
- gate_down: bfloat16 [3, 180, 6], replicated, may hold values from -4 to 4
- gate_up: bfloat16 [3, 6, 180], replicated, may hold values from -6 to 6
- mlp_in: bfloat16 [4, 180, 360], replicated, may hold values from -0.4375 to 0.4375
- mlp_out: bfloat16 [4, 360, 180], replicated, may hold values from -0.3125 to 0.3125
- ocab_qkv: bfloat16 [180, 540], replicated, may hold values from -1.8 to 1.8
- ocab_proj: bfloat16 [180, 180], replicated, may hold values from -0.4375 to 0.4375
Outputs:
- refined: bfloat16 [128, 1024, 180], P('row', 'col')
All inputs are finite; a program needn't handle non-finite values.
Results may differ from a plain program's by a relative error of at most 0.034.
Values may be sent and summed in bfloat16 or wider, within the bound.
A program may use at most 128 MiB of HBM per device.

v0:
```python
import jax
import jax.numpy as jnp
from jax import lax
from jax.experimental import pallas as pl
from jax.experimental.pallas import tpu as pltpu
from jax.sharding import PartitionSpec as P

C = 180
HEADS = 6
HD = C // HEADS
WIN = 16
L = 256
HID = 360
HL = 384
ROWS = 8
COLS = 16
H = 16
W = 64
E = 80
HALO = (2, 8, 2, 4)
EPSILON = 1e-05
BIG = -1e30
QSCALE = HD ** (-0.5) * 1.4426950408889634
F32 = jnp.float32
BF16 = jnp.bfloat16
MESH = pl.DeviceIdType.MESH


def dot(a, b):
    return jnp.dot(a, b, preferred_element_type=F32)


def dot_t(a, b):
    return lax.dot_general(a, b, (((1,), (1,)), ((), ())), preferred_element_type=F32)


def gelu(v):
    return v * (1.0 + lax.erf(v * 0.7071067811865476)) * 0.5


def iota(shape, dim):
    return lax.broadcasted_iota(jnp.int32, shape, dim)


def layer_norm(x):
    nd = x.ndim
    inside = iota((1,) * (nd - 1) + (L,), nd - 1) < C
    mean = jnp.sum(x, axis=-1, keepdims=True) * (1.0 / C)
    centered = jnp.where(inside, x - mean, 0.0)
    spread = jnp.sum(centered * centered, axis=-1, keepdims=True) * (1.0 / C)
    return centered * lax.rsqrt(spread + EPSILON)


def attend(q, k, v, group):
    tq = q.shape[0]
    lane = iota((1, L), 1)
    total = None
    for first in range(0, HEADS, group):
        stacked = []
        for h in range(first, first + group):
            mask = ((lane >= h * HD) & (lane < h * HD + HD)) | (lane >= C)
            stacked.append(q * mask.astype(F32).astype(BF16))
        qm = jnp.concatenate(stacked, axis=0)
        s = dot_t(qm, k)
        p = jnp.exp2(s - jnp.max(s, axis=-1, keepdims=True))
        inv = 1.0 / jnp.sum(p, axis=-1, keepdims=True)
        r = dot(p.astype(BF16), v) * inv
        for i in range(group):
            h = first + i
            mask = (lane >= h * HD) & (lane < h * HD + HD)
            part = jnp.where(mask, r[i * tq : (i + 1) * tq], 0.0)
            total = part if total is None else total + part
    return total.astype(BF16)


def kernel(
    tok, wqkv, wp, w1, w2, gd, gu, m1, m2, out,
    st, un, ue, rl, rr, qs, ks, vs, qe, ke, ve, att, ex, c1, h32, hc, c2, ara, arb,
    hs, hr, asend, arecv, bsend, brecv,
):
    row = lax.axis_index("row")
    col = lax.axis_index("col")
    up, down = lax.rem(row + ROWS - 1, ROWS), lax.rem(row + 1, ROWS)
    left, right = lax.rem(col + COLS - 1, COLS), lax.rem(col + 1, COLS)

    barrier = pltpu.get_barrier_semaphore()
    peers = [(lax.rem(row + d, ROWS), col) for d in range(1, ROWS)]
    peers += [(row, lax.rem(col + d, COLS)) for d in range(1, COLS)]
    peers += [(up, left), (up, right), (down, left), (down, right)]
    for peer in peers:
        pl.semaphore_signal(barrier, inc=1, device_id=peer, device_id_type=MESH)

    st[...] = jnp.zeros_like(st)
    st[:, :, :C] = tok[...].astype(F32)
    pl.semaphore_wait(barrier, len(peers))

    def remote(src, dst, send, recv, peer):
        return pltpu.make_async_remote_copy(
            src_ref=src, dst_ref=dst, send_sem=send, recv_sem=recv, device_id=peer, device_id_type=MESH
        )

    def halo_copies(k):
        n = HALO[k]
        u, a, b = ue.at[k], rl.at[k], rr.at[k]
        top, low = pl.ds(8, n), pl.ds(24 - n, n)
        above, below = pl.ds(8 - n, n), pl.ds(24, n)
        mid = pl.ds(8, H)
        first, last = pl.ds(0, 16), pl.ds(64, 16)
        plan = [
            (u.at[top], u.at[below], (up, col)),
            (u.at[low], u.at[above], (down, col)),
            (u.at[mid, first], b.at[mid], (row, left)),
            (u.at[mid, last], a.at[mid], (row, right)),
            (u.at[top, first], b.at[below], (up, left)),
            (u.at[top, last], a.at[below], (up, right)),
            (u.at[low, first], b.at[above], (down, left)),
            (u.at[low, last], a.at[above], (down, right)),
        ]
        return [remote(s, d, hs.at[k, i], hr.at[k, i], p) for i, (s, d, p) in enumerate(plan)]

    def normalize(k):
        def step(i, carry):
            x = st[pl.ds(i * 8, 8)]
            u = layer_norm(x)
            un[pl.ds(i * 8, 8)] = u.astype(BF16)
            pad = jnp.zeros((8, 8, L), F32)
            ue[k, pl.ds(8 + i * 8, 8)] = jnp.concatenate([pad, u, pad], axis=1).astype(BF16)
            return carry

        lax.fori_loop(0, 2, step, 0)

    def merge(k):
        n = HALO[k]
        rows = pl.ds(8 - n, H + 2 * n)
        half = iota((1, 16, 1), 1) < 8
        a = rl[k, rows].astype(F32)
        t = ue[k, rows, 0:16].astype(F32)
        ue[k, rows, 0:16] = jnp.where(half, a, t).astype(BF16)
        b = rr[k, rows].astype(F32)
        t = ue[k, rows, 64:80].astype(F32)
        ue[k, rows, 64:80] = jnp.where(half, t, b).astype(BF16)

    def clear_outside(k):
        n = HALO[k]
        rows = pl.ds(8 - n, H + 2 * n)

        @pl.when(row == 0)
        def _():
            ue[k, pl.ds(8 - n, n)] = jnp.zeros((n, E, L), BF16)

        @pl.when(row == ROWS - 1)
        def _():
            ue[k, pl.ds(24, n)] = jnp.zeros((n, E, L), BF16)

        half = iota((1, 16, 1), 1) < 8

        @pl.when(col == 0)
        def _():
            t = ue[k, rows, 0:16].astype(F32)
            ue[k, rows, 0:16] = jnp.where(half, 0.0, t).astype(BF16)

        @pl.when(col == COLS - 1)
        def _():
            t = ue[k, rows, 64:80].astype(F32)
            ue[k, rows, 64:80] = jnp.where(half, t, 0.0).astype(BF16)

    def project(k, which, src, dst, rows, width, chunk, at):
        def step(i, carry):
            x = src[pl.ds(at + i * chunk, chunk)].reshape(chunk * width, L)
            y = dot(x, wqkv[k, which])
            if which == 0:
                y = y * QSCALE
            dst[pl.ds(i * chunk, chunk)] = y.astype(BF16).reshape(chunk, width, L)
            return carry

        lax.fori_loop(0, rows // chunk, step, 0)

    def plain_window(k):
        def step(w, carry):
            cols = pl.ds(pl.multiple_of(w * WIN, WIN), WIN)
            q = qs[:, cols].reshape(WIN * WIN, L)
            kk = ks[:, cols].reshape(WIN * WIN, L)
            vv = vs[:, cols].reshape(WIN * WIN, L)
            o = attend(q, kk, vv, HEADS)
            att[:, cols] = dot(o, wp[k]).reshape(WIN, WIN, L)
            return carry

        return step

    def shifted_window(k):
        lane = iota((1, 1, L), 2)
        qcol = iota((8, WIN, 1), 1) >= 8
        qpat = jnp.where(lane == C, 1.0, 0.0) + jnp.where(
            ((lane == C + 1) & ~qcol) | ((lane == C + 2) & qcol), 1.0, 0.0
        )
        krow = iota((WIN, WIN, 1), 0) >= 8
        kcol = iota((WIN, WIN, 1), 1) >= 8

        def step(i, carry):
            ry = i // 5
            w = i - ry * 5
            cols = pl.ds(pl.multiple_of(w * WIN, WIN), WIN)
            split_row = ((ry == 1) & (row == ROWS - 1)) | ((ry == 0) & (row == 0))
            split_col = ((w == 4) & (col == COLS - 1)) | ((w == 0) & (col == 0))
            brow = jnp.where(split_row, BIG, 0.0)
            bcol = jnp.where(split_col, BIG, 0.0)
            other = jnp.where(ry == 0, 0.0, 1.0)
            krf = jnp.where(krow, 1.0, 0.0)
            differs = krf * other + (1.0 - krf) * (1.0 - other)
            bias = jnp.where(lane == C, differs * brow, 0.0) + jnp.where(
                ((lane == C + 1) & kcol) | ((lane == C + 2) & ~kcol), bcol, 0.0
            )
            q = (qe[pl.ds(ry * 8, 8), cols].astype(F32) + qpat).astype(BF16)
            kk = (ke[pl.ds(ry * WIN, WIN), cols].astype(F32) + bias).astype(BF16)
            vv = ve[pl.ds(ry * WIN, WIN), cols]
            o = attend(
                q.reshape(8 * WIN, L), kk.reshape(WIN * WIN, L), vv.reshape(WIN * WIN, L), HEADS
            )
            att[pl.ds(ry * 8, 8), cols] = dot(o, wp[k]).reshape(8, WIN, L)
            return carry

        return step

    def cross_window(k):
        lane = iota((1, 1, L), 2)
        qpat = jnp.where(lane == C, 1.0, 0.0)
        kcol = iota((1, 32, 1), 1)
        bias = jnp.where((lane == C) & ((kcol < 4) | (kcol >= 28)), BIG, 0.0)

        def step(w, carry):
            cols = pl.ds(pl.multiple_of(w * WIN, WIN), WIN)
            wide = pl.ds(pl.multiple_of(w * WIN, WIN), 32)
            q = (qs[:, cols].astype(F32) + qpat).astype(BF16).reshape(WIN * WIN, L)
            kk = (ke[pl.ds(4, 24), wide].astype(F32) + bias).astype(BF16).reshape(24 * 32, L)
            vv = ve[pl.ds(4, 24), wide].reshape(24 * 32, L)
            o = attend(q, kk, vv, 2)
            att[:, cols] = dot(o, wp[k]).reshape(WIN, WIN, L)
            return carry

        return step

    def conv_in(k):
        hrow = iota((6, E, 1), 0)
        hcol = iota((6, E, 1), 1)
        lane = iota((1, 1, 128), 2)
        low = jnp.where(col == 0, 8, 0)
        high = jnp.where(col == COLS - 1, 72, E)
        rlow = jnp.where(row == 0, 1, 0)
        rhigh = jnp.where(row == ROWS - 1, 17, 18)

        def step(i, carry):
            acc = None
            for a in range(3):
                x = ue[k, pl.ds(6 + a + i * 6, 6)].reshape(6 * E, L)
                y = dot(x, w1[k, a])
                acc = y if acc is None else acc + y
            r = acc.reshape(6, E, L)
            first, second = r[:, :, :128], r[:, :, 128:]
            s = pltpu.roll(first, 1, 1) + pltpu.roll(first, 64, 2) + pltpu.roll(second, E - 1, 1)
            g = gelu(s)
            rr_ = hrow + i * 6
            ok = (rr_ >= rlow) & (rr_ < rhigh) & (hcol >= low) & (hcol < high) & (lane < 60)
            h32[pl.ds(i * 6, 6)] = jnp.where(ok, g, 0.0)
            return carry

        lax.fori_loop(0, 3, step, 0)

    def conv_out(k):
        def step(i, total):
            lead = h32[pl.ds(i * 4, 4)]
            mid = h32[pl.ds(i * 4 + 1, 4)]
            tail = h32[pl.ds(i * 4 + 2, 4)]
            x = jnp.concatenate([lead + pltpu.roll(mid, 64, 2), tail], axis=2)
            x = x.astype(BF16).reshape(4 * E, L)
            r0 = dot(x, w2[k, 0]).reshape(4, E, L)
            r1 = dot(x, w2[k, 1]).reshape(4, E, L)
            r2 = dot(x, w2[k, 2]).reshape(4, E, L)
            y = (pltpu.roll(r0, 1, 1) + r1 + pltpu.roll(r2, E - 1, 1))[:, 8:72]
            ex[pl.ds(i * 4, 4)] = y
            return total + jnp.sum(jnp.sum(y, axis=0), axis=0, keepdims=True)

        return lax.fori_loop(0, 4, step, jnp.zeros((1, L), F32))

    def stage_a(k):
        return [
            remote(ara.at[k, 0], ara.at[k, d], asend.at[k, d], arecv.at[k, d], (lax.rem(row + d, ROWS), col))
            for d in range(1, ROWS)
        ]

    def stage_b(k):
        return [
            remote(arb.at[k, 0], arb.at[k, d], bsend.at[k, d], brecv.at[k, d], (row, lax.rem(col + d, COLS)))
            for d in range(1, COLS)
        ]

    def start(copies):
        for c in copies:
            c.start()

    def finish(copies):
        for c in copies:
            c.wait()

    def between(k, copies):
        finish(copies)
        s = ara[k, 0]
        for d in range(1, ROWS):
            s = s + ara[k, d]
        arb[k, 0] = s
        nxt = stage_b(k)
        start(nxt)
        return nxt

    def gate(k, copies):
        finish(copies)
        s = arb[k, 0]
        for d in range(1, COLS):
            s = s + arb[k, d]
        pooled = s * (1.0 / (ROWS * COLS * H * W))
        squeezed = jnp.sum(gd[k] * pooled, axis=-1, keepdims=True)
        squeezed = jnp.maximum(squeezed, 0.0)
        z = jnp.sum(gu[k] * squeezed, axis=0, keepdims=True)
        return 1.0 / (1.0 + jnp.exp(-z))

    def feed_forward(k, scale, offset):
        def step(i, carry):
            rows = pl.ds(i * 4, 4)
            x = st[rows] + att[rows, offset : offset + W]
            if scale is not None:
                x = x + ex[rows] * scale.reshape(1, 1, L)
            u = layer_norm(x).astype(BF16).reshape(4 * W, L)
            h = gelu(dot(u, m1[k])).astype(BF16)
            st[rows] = x + dot(h, m2[k]).reshape(4, W, L)
            return carry

        lax.fori_loop(0, 4, step, 0)

    for k in range(4):
        normalize(k)
        halos = halo_copies(k)
        start(halos)
        if k == 1:
            finish(halos)
            merge(k)
            project(k, 0, ue.at[k], qe, H, E, 4, 8)
            project(k, 1, ue.at[k], ke, 32, E, 4, 0)
            project(k, 2, ue.at[k], ve, 32, E, 4, 0)
            clear_outside(k)
            conv = True
            windows = shifted_window(k)
            cuts = (0, 0, 5, 10)
            offset = 8
        elif k == 3:
            project(k, 0, un, qs, H, W, 4, 0)
            finish(halos)
            merge(k)
            clear_outside(k)
            project(k, 1, ue.at[k, pl.ds(4, 24)], ke.at[pl.ds(4, 24)], 24, E, 4, 0)
            project(k, 2, ue.at[k, pl.ds(4, 24)], ve.at[pl.ds(4, 24)], 24, E, 4, 0)
            conv = False
            windows = cross_window(k)
            cuts = (0, 4)
            offset = 0
        else:
            project(k, 0, un, qs, H, W, 4, 0)
            project(k, 1, un, ks, H, W, 4, 0)
            project(k, 2, un, vs, H, W, 4, 0)
            conv = True
            windows = plain_window(k)
            cuts = (0, 2, 3, 4)
            offset = 0
        lax.fori_loop(cuts[0], cuts[1], windows, 0)
        scale = None
        if conv:
            if k != 1:
                finish(halos)
                merge(k)
                clear_outside(k)
            conv_in(k)
            ara[k, 0] = conv_out(k)
            copies = stage_a(k)
            start(copies)
            lax.fori_loop(cuts[1], cuts[2], windows, 0)
            copies = between(k, copies)
            lax.fori_loop(cuts[2], cuts[3], windows, 0)
            scale = gate(k, copies)
        feed_forward(k, scale, offset)
    out[...] = st[:, :, :C].astype(BF16)


def pad_to(value, *sizes):
    lead = value.ndim - len(sizes)
    return jnp.pad(
        value, [(0, 0)] * lead + [(0, s - n) for s, n in zip(sizes, value.shape[lead:], strict=True)]
    )


def local(tok, qkv, proj, squeeze, expand, down, up, mlp_in, mlp_out, oqkv, oproj):
    wqkv = jnp.concatenate([qkv, oqkv[None]]).reshape(4, C, 3, C).transpose(0, 2, 1, 3)
    wqkv = pad_to(wqkv, L, L)
    wp = pad_to(jnp.concatenate([proj, oproj[None]]), L, L)
    w1 = pad_to(squeeze.reshape(3, 3, 3, C, 60).transpose(0, 1, 3, 2, 4), 64)
    w1 = pad_to(w1.reshape(3, 3, C, 192), L, L)
    w2 = pad_to(expand.reshape(3, 3, 3, 60, C).transpose(0, 2, 1, 3, 4), 64, L)
    w2 = pad_to(w2.reshape(3, 3, 192, L), L, L)
    gd = pad_to(down.transpose(0, 2, 1).astype(F32), 8, L)
    gu = pad_to(up.astype(F32), 8, L)
    m1 = pad_to(mlp_in, L, HL)
    m2 = pad_to(mlp_out, HL, L)
    vmem = pl.BlockSpec(memory_space=pltpu.VMEM)
    return pl.pallas_call(
        kernel,
        out_shape=jax.ShapeDtypeStruct((H, W, C), BF16),
        in_specs=[vmem] * 9,
        out_specs=vmem,
        scratch_shapes=[
            pltpu.VMEM((H, W, L), F32),
            pltpu.VMEM((H, W, L), BF16),
            pltpu.VMEM((4, 32, E, L), BF16),
            pltpu.VMEM((4, 32, 16, L), BF16),
            pltpu.VMEM((4, 32, 16, L), BF16),
            pltpu.VMEM((H, W, L), BF16),
            pltpu.VMEM((H, W, L), BF16),
            pltpu.VMEM((H, W, L), BF16),
            pltpu.VMEM((H, E, L), BF16),
            pltpu.VMEM((32, E, L), BF16),
            pltpu.VMEM((32, E, L), BF16),
            pltpu.VMEM((H, E, L), F32),
            pltpu.VMEM((H, W, L), F32),
            pltpu.VMEM((8, 128), F32),
            pltpu.VMEM((18, E, 128), F32),
            pltpu.VMEM((8, 128), F32),
            pltpu.VMEM((8, 128), F32),
            pltpu.VMEM((3, ROWS, 1, L), F32),
            pltpu.VMEM((3, COLS, 1, L), F32),
            pltpu.SemaphoreType.DMA((4, 8)),
            pltpu.SemaphoreType.DMA((4, 8)),
            pltpu.SemaphoreType.DMA((3, ROWS)),
            pltpu.SemaphoreType.DMA((3, ROWS)),
            pltpu.SemaphoreType.DMA((3, COLS)),
            pltpu.SemaphoreType.DMA((3, COLS)),
        ],
        compiler_params=pltpu.CompilerParams(
            collective_id=0, has_side_effects=True, vmem_limit_bytes=60 * 1024 * 1024
        ),
        name="blocks",
    )(tok, wqkv, wp, w1, w2, gd, gu, m1, m2)


def solution(mesh):
    placed = (P("row", "col", None),) + (P(),) * 10
    return jax.shard_map(
        local, mesh=mesh, in_specs=placed, out_specs=P("row", "col", None), check_vma=False
    )
```

profile of v0, /device:TPU:0, one launch (start us, length us, event | category | flops | bytes accessed | tf_op | source)
XLA Modules:
  0.0 143.3 jit_solution(138020051729698894)
XLA Ops:
  0.0 1.3 pad_convert_fusion
  1.3 2.7 %reshape.20 = bf16[3,180,3,180]{3,2,1,0:T(4,128)(2,1)S(1)} reshape(bf16[3,180,540]{2,1,0:T(8,128)(2,1)} %param.12) | data formatting | bytes 1166400 | tf_op jit(solution)/shard_map/concatenate | solution.py:399
  4.1 0.0 copy-start.5
  4.1 0.1 copy.18
  4.2 0.8 copy-done.5
  5.0 0.2 reshape.21
  5.3 0.2 maximum_bitcast_fusion
  5.5 0.0 copy-start
  5.5 1.4 pad.43.wqkv
  6.9 0.1 copy.29
  7.0 0.2 pad.47
  7.1 1.1 pad.48.w2
  8.3 0.4 copy-done.1
  8.7 0.2 pad.45
  8.8 0.7 copy.20
  9.6 0.0 copy-start.2
  9.6 1.2 pad.46.w1
  10.8 0.9 copy.23
  11.7 1.0 pad.54.m2
  12.7 0.1 copy.22
  12.8 1.0 pad.53.m1
  13.8 0.9 fusion.5.wp
  14.7 126.7 %blocks.1 = bf16[16,64,180]{2,1,0:T(8,128)(2,1)} custom-call(bf16[16,64,180]{2,1,0:T(8,128)(2,1)} %tok.1, bf16[4,3,256,256]{3,2,1,0:T(8,128)(2,1)} %pad.43.wqkv, bf16[4,256,256]{2,1,0:T(8,128)(2,1)} %fusion.5.wp, bf16[3,3,256,256]{3,2,1,0:T(8,128)(2,1)} %pad.46.w1, bf16[3,3,256,256]{3,2,1,0:T(8,128)(2,1)} %pad.48.w2, f32[3,8,256]{2,1,0:T(8,128)} %get-tuple-element.6.gd, ...), custom_call_target="tpu_custom_call" | custom-call | tf_op jit(solution)/shard_map/blocks/pallas_call | solution.py:411
  141.4 1.9 %copy.31 = bf16[16,64,180]{2,1,0:T(8,128)(2,1)} copy(bf16[16,64,180]{2,1,0:T(8,128)(2,1)} %blocks.1) | data formatting | bytes 737280
  (10 shorter events, 0.1 us)
Async XLA Ops:
  4.1 0.9 copy-start.5
  5.5 1.4 copy-start
  7.1 1.5 %copy-start.1 = (bf16[3,9,180,60]{2,3,1,0:T(8,128)(2,1)S(1)}, bf16[3,9,180,60]{2,3,1,0:T(8,128)(2,1)}, u32[]{:S(2)}) copy-start(bf16[3,9,180,60]{2,3,1,0:T(8,128)(2,1)} %param.14) | copy-start | bytes 1749604
  9.6 1.2 copy-start.2
  10.8 1.9 %copy-start.3 = (bf16[4,180,360]{2,0,1:T(4,128)(2,1)S(1)}, bf16[4,180,360]{2,0,1:T(4,128)(2,1)}, u32[]{:S(2)}) copy-start(bf16[4,180,360]{2,0,1:T(4,128)(2,1)} %param.18) | copy-start | bytes 1555204
  12.7 1.1 copy-start.4
  12.7 1.1 copy-start.6
where the time goes:
time: 144 us; the launch traced here: 143 us
  Pallas kernels  127 us (88%)
  local copies, waits for them, and re-layouts  14 us (10%)
  other arithmetic  2.45 us (2%)
    pallas_call x1, Pallas kernels, local(): pl.pallas_call(kernel, out_shape=jax.ShapeDtypeStruct((H, W, C), BF16), i...  127 us
    pad x7, local copies, waits for them, and re-layouts, pad_to(): jnp.pad(value, [(0, 0)] * lead + [(0, s - n) for s, n in zip(sizes, value...  6.06 us
    unnamed x17, local copies, waits for them, and re-layouts  4.09 us
    concatenate x4, local copies, waits for them, and re-layouts, local(): jnp.concatenate([qkv, oqkv[None]]).reshape(4, C, 3, C).transpose(0, 2, 1, 3)  3.08 us

commit v1 on v0

v1 whole, which is shorter than its diff:
```python
import jax
import jax.numpy as jnp
from jax import lax
from jax.experimental import pallas as pl
from jax.experimental.pallas import tpu as pltpu
from jax.sharding import PartitionSpec as P

C = 180
HEADS = 6
HD = C // HEADS
WIN = 16
L = 256
HID = 360
HL = 384
ROWS = 8
COLS = 16
H = 16
W = 64
E = 80
EPSILON = 1e-05
BIG = -1e30
QSCALE = HD ** (-0.5) * 1.4426950408889634
F32 = jnp.float32
BF16 = jnp.bfloat16
MESH = pl.DeviceIdType.MESH
GROUPS = ((0, 2, True), (0, 2, True), (2, 6, False), (0, 2, True), (0, 4, True))


def dot(a, b):
    return jnp.dot(a, b, preferred_element_type=F32)


def dot_t(a, b):
    return lax.dot_general(a, b, (((1,), (1,)), ((), ())), preferred_element_type=F32)


def gelu(v):
    return v * (1.0 + lax.erf(v * 0.7071067811865476)) * 0.5


def iota(shape, dim):
    return lax.broadcasted_iota(jnp.int32, shape, dim)


def layer_norm(x):
    nd = x.ndim
    inside = iota((1,) * (nd - 1) + (L,), nd - 1) < C
    mean = jnp.sum(x, axis=-1, keepdims=True) * (1.0 / C)
    centered = jnp.where(inside, x - mean, 0.0)
    spread = jnp.sum(centered * centered, axis=-1, keepdims=True) * (1.0 / C)
    return centered * lax.rsqrt(spread + EPSILON)


def attend(q, k, v, group):
    tq = q.shape[0]
    lane = iota((1, L), 1)
    total = None
    for first in range(0, HEADS, group):
        stacked = []
        for h in range(first, first + group):
            mask = ((lane >= h * HD) & (lane < h * HD + HD)) | (lane >= C)
            stacked.append(q * mask.astype(F32).astype(BF16))
        qm = jnp.concatenate(stacked, axis=0)
        s = dot_t(qm, k)
        p = jnp.exp2(s - jnp.max(s, axis=-1, keepdims=True))
        inv = 1.0 / jnp.sum(p, axis=-1, keepdims=True)
        r = dot(p.astype(BF16), v) * inv
        for i in range(group):
            h = first + i
            mask = (lane >= h * HD) & (lane < h * HD + HD)
            part = jnp.where(mask, r[i * tq : (i + 1) * tq], 0.0)
            total = part if total is None else total + part
    return total.astype(BF16)


def packed(n):
    return n + (n + 1) // 2


def pack(x, ref):
    n = x.shape[0]
    half = (n + 1) // 2
    ref[0:n] = x[:, :, :128].astype(BF16)
    low = x[:half, :, 128:]
    if n > half:
        high = pltpu.roll(x[half:, :, 128:], 64, 2)
        if n < 2 * half:
            high = jnp.concatenate([high, jnp.zeros_like(low[:1])], axis=0)
        low = low + high
    ref[n : n + half] = low.astype(BF16)


def unpack(ref, n):
    half = (n + 1) // 2
    upper = iota((1, 1, 128), 2) < C - 128
    both = ref[n : n + half].astype(F32)
    b = jnp.where(upper, both, 0.0)
    if n > half:
        high = jnp.where(upper, pltpu.roll(both, 64, 2), 0.0)
        b = jnp.concatenate([b, high[: n - half]], axis=0)
    return jnp.concatenate([ref[0:n].astype(F32), b], axis=2)


def fold(x):
    m = x.shape[0] // 2
    return jnp.concatenate([x[:m], x[m:]], axis=1)


def unfold(x):
    return jnp.concatenate([x[:, :8], x[:, 8:]], axis=0)


def kernel(*refs):
    (
        tok, qkv_h, proj_h, sq_h, ex_h, gd_h, gu_h, m1_h, m2_h, oqkv_h, oproj_h, out,
        rqkv, rproj, rsq, rex, rgd, rgu, rm1, rm2, roqkv, roproj,
        wqkv, wp, w1, w2, gd, gu, m1, m2, tmp,
        st, un, ue, ua, qs, ks, vs, qe, ke, ve, att, ex, h32, ara, arb,
    ) = refs[:46]
    bufs = refs[46 : 46 + 6 * len(GROUPS)]
    wsem, hs, hr, asend, arecv, bsend, brecv = refs[46 + 6 * len(GROUPS) :]
    row_s, row_r, col_s, col_r, cor_s, cor_r = (bufs[i :: 6] for i in range(6))
    row = lax.axis_index("row")
    col = lax.axis_index("col")
    up, down = lax.rem(row + ROWS - 1, ROWS), lax.rem(row + 1, ROWS)
    left, right = lax.rem(col + COLS - 1, COLS), lax.rem(col + 1, COLS)

    barrier = pltpu.get_barrier_semaphore()
    peers = [(lax.rem(row + d, ROWS), col) for d in range(1, ROWS)]
    peers += [(row, lax.rem(col + d, COLS)) for d in range(1, COLS)]
    peers += [(up, left), (up, right), (down, left), (down, right)]
    for peer in peers:
        pl.semaphore_signal(barrier, inc=1, device_id=peer, device_id_type=MESH)

    loads = [
        pltpu.make_async_copy(s, d, wsem.at[i])
        for i, (s, d) in enumerate(
            [
                (qkv_h, rqkv), (proj_h, rproj), (sq_h, rsq), (ex_h, rex), (gd_h, rgd),
                (gu_h, rgu), (m1_h, rm1), (m2_h, rm2), (oqkv_h, roqkv), (oproj_h, roproj),
            ]
        )
    ]
    for c in loads:
        c.start()

    def remote(src, dst, send, recv, peer):
        return pltpu.make_async_remote_copy(
            src_ref=src, dst_ref=dst, send_sem=send, recv_sem=recv, device_id=peer, device_id_type=MESH
        )

    def start(copies):
        for c in copies:
            c.start()

    def finish(copies):
        for c in copies:
            c.wait()


    def prepare_attention(k):
        w = rqkv.at[k] if k < 3 else roqkv
        zero = jnp.zeros((L, L), BF16)
        for i in range(3):
            wqkv[k, i] = zero
        whole = w[...]
        wqkv[k, 0, 0:C, 0:C] = w[:, 0:C]
        for i in range(1, 3):
            pick = (iota((3 * C, L), 0) == iota((3 * C, L), 1) + i * C) & (iota((3 * C, L), 1) < C)
            wqkv[k, i, 0:C] = dot(whole, jnp.where(pick, 1.0, 0.0).astype(BF16)).astype(BF16)
        wp[k] = zero
        wp[k, 0:C, 0:C] = rproj[k] if k < 3 else roproj[...]

    def prepare_conv(k):
        zero = jnp.zeros((L, L), BF16)
        for a in range(3):
            w1[k, a] = zero
            tmp[...] = jnp.zeros_like(tmp)
            tmp[0:C, 0:60] = rsq[k, 3 * a + 1].astype(F32)
            w1[k, a, 0:C, 0:60] = rsq[k, 3 * a]
            w1[k, a, 0:C, 128:188] = rsq[k, 3 * a + 2]
            w1[k, a, :, 0:128] = (w1[k, a, :, 0:128].astype(F32) + pltpu.roll(tmp[...], 64, 1)).astype(BF16)
        for b in range(3):
            w2[k, b] = zero
            for a in range(3):
                w2[k, b, 64 * a : 64 * a + 60, 0:C] = rex[k, 3 * a + b]
        tmp[...] = jnp.zeros_like(tmp)
        tmp[0:C, 0:6] = rgd[k].astype(F32)
        gd[k] = tmp[...].T[0:8]
        gu[k] = jnp.zeros((8, L), F32)
        gu[k, 0:6, 0:C] = rgu[k].astype(F32)

    def prepare_mlp(k):
        m1[k] = jnp.zeros((L, HL), BF16)
        m1[k, 0:C, 0:HID] = rm1[k]
        m2[k] = jnp.zeros((HL, L), BF16)
        m2[k, 0:HID, 0:C] = rm2[k]


    def copies_of(g):
        plan = [
            (row_s[g].at[0], row_r[g].at[0], (up, col)),
            (row_s[g].at[1], row_r[g].at[1], (down, col)),
            (col_s[g].at[0], col_r[g].at[0], (row, left)),
            (col_s[g].at[1], col_r[g].at[1], (row, right)),
            (cor_s[g].at[0], cor_r[g].at[0], (up, left)),
            (cor_s[g].at[1], cor_r[g].at[1], (up, right)),
            (cor_s[g].at[2], cor_r[g].at[2], (down, left)),
            (cor_s[g].at[3], cor_r[g].at[3], (down, right)),
        ]
        return [
            remote(s, d, hs.at[g, i], hr.at[g, i], p)
            for i, (s, d, p) in enumerate(plan)
            if GROUPS[g][2] or i not in (2, 3)
        ]

    def send(g):
        d0, n, sides = GROUPS[g]
        top = un[d0 : d0 + n].astype(F32)
        low = un[H - d0 - n : H - d0].astype(F32)
        pack(top, row_s[g].at[0])
        pack(low, row_s[g].at[1])
        pack(fold(top[:, 0:8]), cor_s[g].at[0])
        pack(fold(top[:, W - 8 : W]), cor_s[g].at[1])
        pack(fold(low[:, 0:8]), cor_s[g].at[2])
        pack(fold(low[:, W - 8 : W]), cor_s[g].at[3])
        if sides:
            pack(fold(un[:, 0:16].astype(F32)[:, 0:8]), col_s[g].at[0])
            pack(fold(un[:, W - 16 : W].astype(F32)[:, 8:16]), col_s[g].at[1])
        halos = copies_of(g)
        start(halos)
        return halos

    yes_up = jnp.where(row > 0, 1.0, 0.0)
    yes_down = jnp.where(row < ROWS - 1, 1.0, 0.0)
    yes_left = jnp.where(col > 0, 1.0, 0.0)
    yes_right = jnp.where(col < COLS - 1, 1.0, 0.0)

    def receive(g, masked, whole):
        d0, n, sides = GROUPS[g]
        m = n // 2
        for which, lc, rc, at, keep in ((1, 3, 2, 8 - d0 - n, yes_up), (0, 1, 0, 24 + d0, yes_down)):
            mid = unpack(row_r[g].at[which], n)
            lcorner = unfold(unpack(cor_r[g].at[lc], m))
            rcorner = unfold(unpack(cor_r[g].at[rc], m))
            if whole is not None:
                whole[at : at + n] = jnp.concatenate([lcorner, mid, rcorner], axis=1).astype(BF16)
            if masked is not None:
                masked[at : at + n] = jnp.concatenate(
                    [lcorner * (keep * yes_left), mid * keep, rcorner * (keep * yes_right)], axis=1
                ).astype(BF16)
        if sides:
            lside = unfold(unpack(col_r[g].at[1], 8))
            rside = unfold(unpack(col_r[g].at[0], 8))
            first = un[:, 0:16].astype(F32)[:, 0:8]
            last = un[:, W - 16 : W].astype(F32)[:, 8:16]
            if whole is not None:
                whole[8:24, 0:16] = jnp.concatenate([lside, first], axis=1).astype(BF16)
                whole[8:24, 64:80] = jnp.concatenate([last, rside], axis=1).astype(BF16)
            if masked is not None:
                masked[8:24, 0:16] = jnp.concatenate([lside * yes_left, first], axis=1).astype(BF16)
                masked[8:24, 64:80] = jnp.concatenate([last, rside * yes_right], axis=1).astype(BF16)

    def normalize(k):
        def step(i, carry):
            u = layer_norm(st[pl.ds(i * 8, 8)])
            un[pl.ds(i * 8, 8)] = u.astype(BF16)
            inner = u[:, 8:56].astype(BF16)
            ue[pl.ds(8 + i * 8, 8), 16:64] = inner
            if k == 1:
                ua[pl.ds(8 + i * 8, 8), 16:64] = inner
            return carry

        lax.fori_loop(0, 2, step, 0)

    def project(k, src, targets, first, rows, width, chunk):
        def step(i, carry):
            at = pl.ds(first + i * chunk, chunk)
            x = src[at].reshape(chunk * width, L)
            for which, dst, base in targets:
                y = dot(x, wqkv[k, which])
                if which == 0:
                    y = y * QSCALE
                dst[pl.ds(first - base + i * chunk, chunk)] = y.astype(BF16).reshape(chunk, width, L)
            return carry

        lax.fori_loop(0, rows // chunk, step, 0)


    def plain_window(k):
        def step(w, carry):
            cols = pl.ds(pl.multiple_of(w * WIN, WIN), WIN)
            q = qs[:, cols].reshape(WIN * WIN, L)
            kk = ks[:, cols].reshape(WIN * WIN, L)
            vv = vs[:, cols].reshape(WIN * WIN, L)
            o = attend(q, kk, vv, HEADS)
            att[:, cols] = dot(o, wp[k]).reshape(WIN, WIN, L)
            return carry

        return step

    def shifted_window(k):
        lane = iota((1, 1, L), 2)
        qcol = iota((8, WIN, 1), 1) >= 8
        qpat = jnp.where(lane == C, 1.0, 0.0) + jnp.where(
            ((lane == C + 1) & ~qcol) | ((lane == C + 2) & qcol), 1.0, 0.0
        )
        krow = iota((WIN, WIN, 1), 0) >= 8
        kcol = iota((WIN, WIN, 1), 1) >= 8

        def step(i, carry):
            ry = i // 5
            w = i - ry * 5
            cols = pl.ds(pl.multiple_of(w * WIN, WIN), WIN)
            split_row = ((ry == 1) & (row == ROWS - 1)) | ((ry == 0) & (row == 0))
            split_col = ((w == 4) & (col == COLS - 1)) | ((w == 0) & (col == 0))
            brow = jnp.where(split_row, BIG, 0.0)
            bcol = jnp.where(split_col, BIG, 0.0)
            other = jnp.where(ry == 0, 0.0, 1.0)
            krf = jnp.where(krow, 1.0, 0.0)
            differs = krf * other + (1.0 - krf) * (1.0 - other)
            bias = jnp.where(lane == C, differs * brow, 0.0) + jnp.where(
                ((lane == C + 1) & kcol) | ((lane == C + 2) & ~kcol), bcol, 0.0
            )
            q = (qe[pl.ds(ry * 8, 8), cols].astype(F32) + qpat).astype(BF16)
            kk = (ke[pl.ds(ry * WIN, WIN), cols].astype(F32) + bias).astype(BF16)
            vv = ve[pl.ds(ry * WIN, WIN), cols]
            o = attend(
                q.reshape(8 * WIN, L), kk.reshape(WIN * WIN, L), vv.reshape(WIN * WIN, L), HEADS
            )
            att[pl.ds(ry * 8, 8), cols] = dot(o, wp[k]).reshape(8, WIN, L)
            return carry

        return step

    def cross_window(k):
        lane = iota((1, 1, L), 2)
        qpat = jnp.where(lane == C, 1.0, 0.0)
        kcol = iota((1, 32, 1), 1)
        bias = jnp.where((lane == C) & ((kcol < 4) | (kcol >= 28)), BIG, 0.0)

        def step(w, carry):
            cols = pl.ds(pl.multiple_of(w * WIN, WIN), WIN)
            wide = pl.ds(pl.multiple_of(w * WIN, WIN), 32)
            q = (qs[:, cols].astype(F32) + qpat).astype(BF16).reshape(WIN * WIN, L)
            kk = (ke[pl.ds(4, 24), wide].astype(F32) + bias).astype(BF16).reshape(24 * 32, L)
            vv = ve[pl.ds(4, 24), wide].reshape(24 * 32, L)
            o = attend(q, kk, vv, 2)
            att[:, cols] = dot(o, wp[k]).reshape(WIN, WIN, L)
            return carry

        return step


    def conv_in(k):
        chunk = 9
        hrow = iota((chunk, E, 1), 0)
        hcol = iota((chunk, E, 1), 1)
        lane = iota((1, 1, 128), 2)
        low = jnp.where(col == 0, 8, 0)
        high = jnp.where(col == COLS - 1, 72, E)
        rlow = jnp.where(row == 0, 1, 0)
        rhigh = jnp.where(row == ROWS - 1, 17, 18)

        def step(i, carry):
            acc = None
            for a in range(3):
                x = ue[pl.ds(6 + a + i * chunk, chunk)].reshape(chunk * E, L)
                y = dot(x, w1[k, a])
                acc = y if acc is None else acc + y
            r = acc.reshape(chunk, E, L)
            first, second = r[:, :, :128], r[:, :, 128:]
            s = pltpu.roll(first, 1, 1) + pltpu.roll(first, 64, 2) + pltpu.roll(second, E - 1, 1)
            g = gelu(s)
            at = hrow + i * chunk
            ok = (at >= rlow) & (at < rhigh) & (hcol >= low) & (hcol < high) & (lane < 60)
            h32[pl.ds(i * chunk, chunk)] = jnp.where(ok, g, 0.0)
            return carry

        lax.fori_loop(0, 18 // chunk, step, 0)

    def conv_out(k):
        chunk = 8

        def step(i, total):
            lead = h32[pl.ds(i * chunk, chunk)]
            mid = h32[pl.ds(i * chunk + 1, chunk)]
            tail = h32[pl.ds(i * chunk + 2, chunk)]
            x = jnp.concatenate([lead + pltpu.roll(mid, 64, 2), tail], axis=2)
            x = x.astype(BF16).reshape(chunk * E, L)
            r0 = dot(x, w2[k, 0]).reshape(chunk, E, L)
            r1 = dot(x, w2[k, 1]).reshape(chunk, E, L)
            r2 = dot(x, w2[k, 2]).reshape(chunk, E, L)
            y = (pltpu.roll(r0, 1, 1) + r1 + pltpu.roll(r2, E - 1, 1))[:, 8:72]
            ex[pl.ds(i * chunk, chunk)] = y
            return total + jnp.sum(jnp.sum(y, axis=0), axis=0, keepdims=True)

        return lax.fori_loop(0, H // chunk, step, jnp.zeros((1, L), F32))


    def stage_a(k):
        return [
            remote(ara.at[k, 0], ara.at[k, d], asend.at[k, d], arecv.at[k, d], (lax.rem(row + d, ROWS), col))
            for d in range(1, ROWS)
        ]

    def stage_b(k):
        return [
            remote(arb.at[k, 0], arb.at[k, d], bsend.at[k, d], brecv.at[k, d], (row, lax.rem(col + d, COLS)))
            for d in range(1, COLS)
        ]

    def between(k, copies):
        finish(copies)
        s = ara[k, 0]
        for d in range(1, ROWS):
            s = s + ara[k, d]
        arb[k, 0] = s
        nxt = stage_b(k)
        start(nxt)
        return nxt

    def gate(k, copies):
        finish(copies)
        s = arb[k, 0]
        for d in range(1, COLS):
            s = s + arb[k, d]
        pooled = s * (1.0 / (ROWS * COLS * H * W))
        squeezed = jnp.sum(gd[k] * pooled, axis=-1, keepdims=True)
        squeezed = jnp.maximum(squeezed, 0.0)
        z = jnp.sum(gu[k] * squeezed, axis=0, keepdims=True)
        return 1.0 / (1.0 + jnp.exp(-z))

    def feed_forward(k, scale, offset):
        chunk = 8

        def step(i, carry):
            rows = pl.ds(i * chunk, chunk)
            x = st[rows] + att[rows, offset : offset + W]
            if scale is not None:
                x = x + ex[rows] * scale.reshape(1, 1, L)
            u = layer_norm(x).astype(BF16).reshape(chunk * W, L)
            h = gelu(dot(u, m1[k])).astype(BF16)
            st[rows] = x + dot(h, m2[k]).reshape(chunk, W, L)
            return carry

        lax.fori_loop(0, H // chunk, step, 0)

    st[...] = jnp.zeros_like(st)
    st[:, :, :C] = tok[...].astype(F32)

    normalize(0)
    pl.semaphore_wait(barrier, len(peers))
    halos = send(0)
    finish(loads)
    prepare_attention(0)
    prepare_conv(0)
    project(0, un, ((0, qs, 0), (1, ks, 0), (2, vs, 0)), 0, H, W, 8)
    lax.fori_loop(0, 1, plain_window(0), 0)
    finish(halos)
    receive(0, ue, None)
    conv_in(0)
    ara[0, 0] = conv_out(0)
    copies = stage_a(0)
    start(copies)
    lax.fori_loop(1, 4, plain_window(0), 0)
    copies = between(0, copies)
    for k in range(4):
        prepare_mlp(k)
    for k in range(1, 4):
        prepare_attention(k)
    for k in range(1, 3):
        prepare_conv(k)
    feed_forward(0, gate(0, copies), 0)

    normalize(1)
    halos = send(1)
    more = send(2)
    finish(halos)
    receive(1, ue, ua)
    conv_in(1)
    ara[1, 0] = conv_out(1)
    copies = stage_a(1)
    start(copies)
    project(1, ua, ((0, qe, 8), (1, ke, 0), (2, ve, 0)), 8, H, E, 4)
    copies = between(1, copies)
    finish(more)
    receive(2, None, ua)
    project(1, ua, ((1, ke, 0), (2, ve, 0)), 0, 8, E, 4)
    project(1, ua, ((1, ke, 0), (2, ve, 0)), 24, 8, E, 4)
    lax.fori_loop(0, 10, shifted_window(1), 0)
    feed_forward(1, gate(1, copies), 8)

    normalize(2)
    halos = send(3)
    project(2, un, ((0, qs, 0), (1, ks, 0), (2, vs, 0)), 0, H, W, 8)
    lax.fori_loop(0, 2, plain_window(2), 0)
    finish(halos)
    receive(3, ue, None)
    conv_in(2)
    ara[2, 0] = conv_out(2)
    copies = stage_a(2)
    start(copies)
    lax.fori_loop(2, 4, plain_window(2), 0)
    copies = between(2, copies)
    feed_forward(2, gate(2, copies), 0)

    normalize(3)
    halos = send(4)
    project(3, un, ((0, qs, 0),), 0, H, W, 8)
    finish(halos)
    receive(4, ue, None)
    project(3, ue, ((1, ke, 0), (2, ve, 0)), 4, 24, E, 6)
    lax.fori_loop(0, 4, cross_window(3), 0)
    feed_forward(3, None, 0)
    out[...] = st[:, :, :C].astype(BF16)


def local(*args):
    vmem = pl.BlockSpec(memory_space=pltpu.VMEM)
    hbm = pl.BlockSpec(memory_space=pltpu.HBM)
    scratch = [pltpu.VMEM(a.shape, a.dtype) for a in args[1:]]
    scratch += [
        pltpu.VMEM((4, 3, L, L), BF16),
        pltpu.VMEM((4, L, L), BF16),
        pltpu.VMEM((3, 3, L, L), BF16),
        pltpu.VMEM((3, 3, L, L), BF16),
        pltpu.VMEM((3, 8, L), F32),
        pltpu.VMEM((3, 8, L), F32),
        pltpu.VMEM((4, L, HL), BF16),
        pltpu.VMEM((4, HL, L), BF16),
        pltpu.VMEM((L, 128), F32),
        pltpu.VMEM((H, W, L), F32),
        pltpu.VMEM((H, W, L), BF16),
        pltpu.VMEM((32, E, L), BF16),
        pltpu.VMEM((32, E, L), BF16),
        pltpu.VMEM((H, W, L), BF16),
        pltpu.VMEM((H, W, L), BF16),
        pltpu.VMEM((H, W, L), BF16),
        pltpu.VMEM((H, E, L), BF16),
        pltpu.VMEM((32, E, L), BF16),
        pltpu.VMEM((32, E, L), BF16),
        pltpu.VMEM((H, E, L), F32),
        pltpu.VMEM((H, W, L), F32),
        pltpu.VMEM((18, E, 128), F32),
        pltpu.VMEM((3, ROWS, 1, L), F32),
        pltpu.VMEM((3, COLS, 1, L), F32),
    ]
    for _, n, _ in GROUPS:
        for shape in ((2, packed(n), W, 128), (2, packed(8), 16, 128), (4, packed(n // 2), 16, 128)):
            scratch += [pltpu.VMEM(shape, BF16)] * 2
    dma = pltpu.SemaphoreType.DMA
    scratch += [dma((10,)), dma((len(GROUPS), 8)), dma((len(GROUPS), 8))]
    scratch += [dma((3, ROWS)), dma((3, ROWS)), dma((3, COLS)), dma((3, COLS))]
    return pl.pallas_call(
        kernel,
        out_shape=jax.ShapeDtypeStruct((H, W, C), BF16),
        in_specs=[vmem] + [hbm] * 10,
        out_specs=vmem,
        scratch_shapes=scratch,
        compiler_params=pltpu.CompilerParams(
            collective_id=0, has_side_effects=True, vmem_limit_bytes=60 * 1024 * 1024
        ),
        name="blocks",
    )(*args)


def solution(mesh):
    placed = (P("row", "col", None),) + (P(),) * 10
    return jax.shard_map(
        local, mesh=mesh, in_specs=placed, out_specs=P("row", "col", None), check_vma=False
    )
```

time: 144 us -> 103 us (0.72)
  Pallas kernels: 127 us -> 92.7 us
  local copies, waits for them, and re-layouts: 14 us -> 8.76 us
  other arithmetic: 2.45 us -> 0 us
    pallas_call x1, Pallas kernels: 127 us -> 92.7 us  [local(): pl.pallas_call(kernel, out_shape=jax.ShapeDtypeStruct((H, W, C), BF16), i...]
    pad x7 -> x0, local copies, waits for them, and re-layouts: 6.06 us -> none  [pad_to(): jnp.pad(value, [(0, 0)] * lead + [(0, s - n) for s, n in zip(sizes, value...]
    unnamed x17 -> x9, local copies, waits for them, and re-layouts: 4.09 us -> 8.76 us
    concatenate x4 -> x0, local copies, waits for them, and re-layouts: 3.08 us -> none  [local(): jnp.concatenate([qkv, oqkv[None]]).reshape(4, C, 3, C).transpose(0, 2, 1, 3)]
where the time goes in v1:
time: 103 us; the launch traced here: 101 us
  Pallas kernels  92.7 us (90%)
  local copies, waits for them, and re-layouts  8.76 us (9%)
    pallas_call x1, Pallas kernels, local(): pl.pallas_call(kernel, out_shape=jax.ShapeDtypeStruct((H, W, C), BF16), i...  92.7 us
    unnamed x9, local copies, waits for them, and re-layouts  8.76 us

profile of v1, /device:TPU:0, one launch (start us, length us, event | category | flops | bytes accessed | tf_op | source)
XLA Modules:
  0.0 101.5 jit_solution(302227832885294879)
XLA Ops:
  0.0 0.0 copy-start.1
  0.0 0.0 copy-start
  0.0 1.6 %copy.13.refs_5_ = bf16[3,180,6]{2,1,0:T(8,128)(2,1)} copy(bf16[3,180,6]{1,2,0:T(8,128)(2,1)} %param.16) | data formatting | bytes 12960 | tf_op args[5]
  1.6 1.9 %copy.14.refs_7_ = bf16[4,180,360]{2,1,0:T(8,128)(2,1)} copy(bf16[4,180,360]{2,0,1:T(4,128)(2,1)} %param.18) | data formatting | bytes 1036800 | tf_op args[7]
  3.6 0.0 copy-done.1
  3.6 1.6 %copy.15.refs_8_ = bf16[4,360,180]{2,1,0:T(8,128)(2,1)} copy(bf16[4,360,180]{1,0,2:T(4,128)(2,1)S(1)} %copy-done.1) | data formatting | bytes 1036800 | tf_op args[8]
  5.1 0.0 copy-done
  5.1 1.7 %copy.12.refs_3_ = bf16[3,9,180,60]{3,2,1,0:T(8,128)(2,1)} copy(bf16[3,9,180,60]{2,3,1,0:T(8,128)(2,1)S(1)} %copy-done) | data formatting | bytes 1166400 | tf_op args[3]
  6.9 92.7 %blocks.1 = bf16[16,64,180]{2,1,0:T(8,128)(2,1)} custom-call(bf16[16,64,180]{2,1,0:T(8,128)(2,1)} %refs_0_.1, bf16[3,180,540]{2,1,0:T(8,128)(2,1)} %refs_1_.1, bf16[3,180,180]{2,1,0:T(8,128)(2,1)} %refs_2_.1, bf16[3,9,180,60]{3,2,1,0:T(8,128)(2,1)} %copy.12.refs_3_, bf16[3,9,60,180]{3,2,1,0:T(8,128)(2,1)} %refs_4_.1, bf16[3,180,6]{2,1,0:T(8,128)(2,1)} %copy.13.refs_5_, ...), custom_call_target="tpu_custom_call" | custom-call | tf_op jit(solution)/shard_map/blocks/pallas_call | solution.py:555
  99.6 1.9 %copy.17 = bf16[16,64,180]{2,1,0:T(8,128)(2,1)} copy(bf16[16,64,180]{2,1,0:T(8,128)(2,1)} %blocks.1) | data formatting | bytes 737280
Async XLA Ops:
  0.0 3.6 %copy-start.1 = (bf16[4,360,180]{1,0,2:T(4,128)(2,1)S(1)}, bf16[4,360,180]{1,0,2:T(4,128)(2,1)}, u32[]{:S(2)}) copy-start(bf16[4,360,180]{1,0,2:T(4,128)(2,1)} %param.19) | copy-start | bytes 1555204
  0.0 5.1 %copy-start = (bf16[3,9,180,60]{2,3,1,0:T(8,128)(2,1)S(1)}, bf16[3,9,180,60]{2,3,1,0:T(8,128)(2,1)}, u32[]{:S(2)}) copy-start(bf16[3,9,180,60]{2,3,1,0:T(8,128)(2,1)} %param.14) | copy-start | bytes 1749604

commit v2 on v1

--- a/solution.py
+++ b/solution.py
@@ -51,26 +51,41 @@
     return centered * lax.rsqrt(spread + EPSILON)
 
 
-def attend(q, k, v, group):
+def attend_part(q, k, v, group):
     tq = q.shape[0]
     lane = iota((1, L), 1)
-    total = None
+    num = top = den = None
     for first in range(0, HEADS, group):
         stacked = []
         for h in range(first, first + group):
             mask = ((lane >= h * HD) & (lane < h * HD + HD)) | (lane >= C)
             stacked.append(q * mask.astype(F32).astype(BF16))
-        qm = jnp.concatenate(stacked, axis=0)
-        s = dot_t(qm, k)
-        p = jnp.exp2(s - jnp.max(s, axis=-1, keepdims=True))
-        inv = 1.0 / jnp.sum(p, axis=-1, keepdims=True)
-        r = dot(p.astype(BF16), v) * inv
+        s = dot_t(jnp.concatenate(stacked, axis=0), k)
+        m = jnp.max(s, axis=-1, keepdims=True)
+        p = jnp.exp2(s - m)
+        d = jnp.sum(p, axis=-1, keepdims=True)
+        r = dot(p.astype(BF16), v)
         for i in range(group):
-            h = first + i
-            mask = (lane >= h * HD) & (lane < h * HD + HD)
-            part = jnp.where(mask, r[i * tq : (i + 1) * tq], 0.0)
-            total = part if total is None else total + part
-    return total.astype(BF16)
+            span = slice(i * tq, (i + 1) * tq)
+            here = lane >= (first + i) * HD
+            wide = [r[span], jnp.broadcast_to(m[span], (tq, L)), jnp.broadcast_to(d[span], (tq, L))]
+            if num is None:
+                num, top, den = wide
+            else:
+                num, top, den = (jnp.where(here, x, y) for x, y in zip(wide, (num, top, den)))
+    return num, top, den
+
+
+def attend(q, k, v, group):
+    num, _, den = attend_part(q, k, v, group)
+    return (num / den).astype(BF16)
+
+
+def merge_parts(a, b):
+    (n0, m0, d0), (n1, m1, d1) = a, b
+    m = jnp.maximum(m0, m1)
+    c0, c1 = jnp.exp2(m0 - m), jnp.exp2(m1 - m)
+    return ((n0 * c0 + n1 * c1) / (d0 * c0 + d1 * c1)).astype(BF16)
 
 
 def packed(n):
@@ -114,11 +129,11 @@
     (
         tok, qkv_h, proj_h, sq_h, ex_h, gd_h, gu_h, m1_h, m2_h, oqkv_h, oproj_h, out,
         rqkv, rproj, rsq, rex, rgd, rgu, rm1, rm2, roqkv, roproj,
-        wqkv, wp, w1, w2, gd, gu, m1, m2, tmp,
+        wqkv, wp, w1, w2, gd, gu, m1, m2, tmp, pn, pm, pd,
         st, un, ue, ua, qs, ks, vs, qe, ke, ve, att, ex, h32, ara, arb,
-    ) = refs[:46]
-    bufs = refs[46 : 46 + 6 * len(GROUPS)]
-    wsem, hs, hr, asend, arecv, bsend, brecv = refs[46 + 6 * len(GROUPS) :]
+    ) = refs[:49]
+    bufs = refs[49 : 49 + 6 * len(GROUPS)]
+    wsem, hs, hr, asend, arecv, bsend, brecv = refs[49 + 6 * len(GROUPS) :]
     row_s, row_r, col_s, col_r, cor_s, cor_r = (bufs[i :: 6] for i in range(6))
     row = lax.axis_index("row")
     col = lax.axis_index("col")
@@ -174,30 +189,27 @@
     def prepare_conv(k):
         zero = jnp.zeros((L, L), BF16)
         for a in range(3):
-            w1[k, a] = zero
-            tmp[...] = jnp.zeros_like(tmp)
-            tmp[0:C, 0:60] = rsq[k, 3 * a + 1].astype(F32)
-            w1[k, a, 0:C, 0:60] = rsq[k, 3 * a]
-            w1[k, a, 0:C, 128:188] = rsq[k, 3 * a + 2]
-            w1[k, a, :, 0:128] = (w1[k, a, :, 0:128].astype(F32) + pltpu.roll(tmp[...], 64, 1)).astype(BF16)
+            tmp[:, 0:L] = zero
+            for b in range(3):
+                tmp[64 * b : 64 * b + 60, 0:C] = rsq[k, 3 * a + b]
+            w1[k, a] = tmp[:, 0:L].astype(F32).T.astype(BF16)
         for b in range(3):
             w2[k, b] = zero
             for a in range(3):
                 w2[k, b, 64 * a : 64 * a + 60, 0:C] = rex[k, 3 * a + b]
-        tmp[...] = jnp.zeros_like(tmp)
-        tmp[0:C, 0:6] = rgd[k].astype(F32)
-        gd[k] = tmp[...].T[0:8]
-        gu[k] = jnp.zeros((8, L), F32)
-        gu[k, 0:6, 0:C] = rgu[k].astype(F32)
+        for dst, raw in ((gd, rgd), (gu, rgu)):
+            dst[k] = jnp.zeros((8, L), F32)
+            dst[k, 0:6, 0:C] = raw[k].astype(F32)
 
     def prepare_mlp(k):
         m1[k] = jnp.zeros((L, HL), BF16)
-        m1[k, 0:C, 0:HID] = rm1[k]
-        m2[k] = jnp.zeros((HL, L), BF16)
-        m2[k, 0:HID, 0:C] = rm2[k]
-
-
-    def copies_of(g):
+        m1[k, 0:C, 0:HID] = rm1[:, k, :]
+        tmp[...] = jnp.zeros((L, HL), BF16)
+        tmp[0:C, 0:HID] = rm2[:, k, :]
+        m2[k] = tmp[...].astype(F32).T.astype(BF16)
+
+
+    def copies_of(g, which):
         plan = [
             (row_s[g].at[0], row_r[g].at[0], (up, col)),
             (row_s[g].at[1], row_r[g].at[1], (down, col)),
@@ -211,11 +223,11 @@
         return [
             remote(s, d, hs.at[g, i], hr.at[g, i], p)
             for i, (s, d, p) in enumerate(plan)
-            if GROUPS[g][2] or i not in (2, 3)
+            if i in which
         ]
 
-    def send(g):
-        d0, n, sides = GROUPS[g]
+    def send_rows(g):
+        d0, n, _ = GROUPS[g]
         top = un[d0 : d0 + n].astype(F32)
         low = un[H - d0 - n : H - d0].astype(F32)
         pack(top, row_s[g].at[0])
@@ -224,20 +236,24 @@
         pack(fold(top[:, W - 8 : W]), cor_s[g].at[1])
         pack(fold(low[:, 0:8]), cor_s[g].at[2])
         pack(fold(low[:, W - 8 : W]), cor_s[g].at[3])
-        if sides:
-            pack(fold(un[:, 0:16].astype(F32)[:, 0:8]), col_s[g].at[0])
-            pack(fold(un[:, W - 16 : W].astype(F32)[:, 8:16]), col_s[g].at[1])
-        halos = copies_of(g)
-        start(halos)
-        return halos
+        rows = copies_of(g, (0, 1, 4, 5, 6, 7))
+        start(rows)
+        return rows
+
+    def send_sides(g):
+        pack(fold(un[:, 0:16].astype(F32)[:, 0:8]), col_s[g].at[0])
+        pack(fold(un[:, W - 16 : W].astype(F32)[:, 8:16]), col_s[g].at[1])
+        sides = copies_of(g, (2, 3))
+        start(sides)
+        return sides
 
     yes_up = jnp.where(row > 0, 1.0, 0.0)
     yes_down = jnp.where(row < ROWS - 1, 1.0, 0.0)
     yes_left = jnp.where(col > 0, 1.0, 0.0)
     yes_right = jnp.where(col < COLS - 1, 1.0, 0.0)
 
-    def receive(g, masked, whole):
-        d0, n, sides = GROUPS[g]
+    def receive_rows(g, masked, whole):
+        d0, n, _ = GROUPS[g]
         m = n // 2
         for which, lc, rc, at, keep in ((1, 3, 2, 8 - d0 - n, yes_up), (0, 1, 0, 24 + d0, yes_down)):
             mid = unpack(row_r[g].at[which], n)
@@ -249,42 +265,66 @@
                 masked[at : at + n] = jnp.concatenate(
                     [lcorner * (keep * yes_left), mid * keep, rcorner * (keep * yes_right)], axis=1
                 ).astype(BF16)
-        if sides:
-            lside = unfold(unpack(col_r[g].at[1], 8))
-            rside = unfold(unpack(col_r[g].at[0], 8))
-            first = un[:, 0:16].astype(F32)[:, 0:8]
-            last = un[:, W - 16 : W].astype(F32)[:, 8:16]
-            if whole is not None:
-                whole[8:24, 0:16] = jnp.concatenate([lside, first], axis=1).astype(BF16)
-                whole[8:24, 64:80] = jnp.concatenate([last, rside], axis=1).astype(BF16)
-            if masked is not None:
-                masked[8:24, 0:16] = jnp.concatenate([lside * yes_left, first], axis=1).astype(BF16)
-                masked[8:24, 64:80] = jnp.concatenate([last, rside * yes_right], axis=1).astype(BF16)
-
-    def normalize(k):
+
+    def receive_sides(g, masked, whole):
+        lside = unfold(unpack(col_r[g].at[1], 8))
+        rside = unfold(unpack(col_r[g].at[0], 8))
+        first = un[:, 0:16].astype(F32)[:, 0:8]
+        last = un[:, W - 16 : W].astype(F32)[:, 8:16]
+        if whole is not None:
+            whole[8:24, 0:16] = jnp.concatenate([lside, first], axis=1).astype(BF16)
+            whole[8:24, 64:80] = jnp.concatenate([last, rside], axis=1).astype(BF16)
+        if masked is not None:
+            masked[8:24, 0:16] = jnp.concatenate([lside * yes_left, first], axis=1).astype(BF16)
+            masked[8:24, 64:80] = jnp.concatenate([last, rside * yes_right], axis=1).astype(BF16)
+
+    def normalize(k, y, rows):
+        u = layer_norm(y)
+        un[rows] = u.astype(BF16)
+        inner = u[:, 8:56].astype(BF16)
+        at = pl.ds(rows.start + 8, rows.size)
+        ue[at, 16:64] = inner
+        if k == 1:
+            ua[at, 16:64] = inner
+
+    def project(k, which, x):
+        r, c, _ = x.shape
+        y = dot(x.reshape(r * c, L), wqkv[k, which])
+        if which == 0:
+            y = y * QSCALE
+        return y.astype(BF16).reshape(r, c, L)
+
+    def project_plain(k, dsts):
         def step(i, carry):
-            u = layer_norm(st[pl.ds(i * 8, 8)])
-            un[pl.ds(i * 8, 8)] = u.astype(BF16)
-            inner = u[:, 8:56].astype(BF16)
-            ue[pl.ds(8 + i * 8, 8), 16:64] = inner
-            if k == 1:
-                ua[pl.ds(8 + i * 8, 8), 16:64] = inner
+            rows = pl.ds(i * 8, 8)
+            x = un[rows]
+            for which, dst in enumerate(dsts):
+                dst[rows] = project(k, which, x)
             return carry
 
         lax.fori_loop(0, 2, step, 0)
 
-    def project(k, src, targets, first, rows, width, chunk):
+    def project_inner(k, src, dsts):
         def step(i, carry):
-            at = pl.ds(first + i * chunk, chunk)
-            x = src[at].reshape(chunk * width, L)
-            for which, dst, base in targets:
-                y = dot(x, wqkv[k, which])
-                if which == 0:
-                    y = y * QSCALE
-                dst[pl.ds(first - base + i * chunk, chunk)] = y.astype(BF16).reshape(chunk, width, L)
-            return carry
-
-        lax.fori_loop(0, rows // chunk, step, 0)
+            x = src[pl.ds(8 + 8 * i, 8), 16:64]
+            for which, dst, base in dsts:
+                dst[pl.ds(8 - base + 8 * i, 8), 16:64] = project(k, which, x)
+            return carry
+
+        lax.fori_loop(0, 2, step, 0)
+
+    def project_sides(k, src, dsts):
+        x = jnp.concatenate([src[8:24, 0:16], src[8:24, 64:80]], axis=1)
+        for which, dst, base in dsts:
+            y = project(k, which, x)
+            dst[8 - base : 24 - base, 0:16] = y[:, 0:16]
+            dst[8 - base : 24 - base, 64:80] = y[:, 16:32]
+
+    def project_rows(k, src, n):
+        for at in (8 - n, 24):
+            x = src[at : at + n]
+            for which, dst in ((1, ke), (2, ve)):
+                dst[at : at + n] = project(k, which, x)
 
 
     def plain_window(k):
@@ -299,53 +339,82 @@
 
         return step
 
-    def shifted_window(k):
+    def keep_part(at, part):
+        for ref, value in zip((pn, pm, pd), part):
+            ref[at] = value.reshape(at.size, 128, L)
+
+    def kept_part(at):
+        return tuple(ref[at].reshape(at.size * 128, L) for ref in (pn, pm, pd))
+
+    def shifted_part(k, ry, w, near):
         lane = iota((1, 1, L), 2)
         qcol = iota((8, WIN, 1), 1) >= 8
         qpat = jnp.where(lane == C, 1.0, 0.0) + jnp.where(
             ((lane == C + 1) & ~qcol) | ((lane == C + 2) & qcol), 1.0, 0.0
         )
-        krow = iota((WIN, WIN, 1), 0) >= 8
-        kcol = iota((WIN, WIN, 1), 1) >= 8
-
+        kcol = iota((8, WIN, 1), 1) >= 8
+        cols = pl.ds(pl.multiple_of(w * WIN, WIN), WIN)
+        split_row = ((ry == 1) & (row == ROWS - 1)) | ((ry == 0) & (row == 0))
+        split_col = ((w == 4) & (col == COLS - 1)) | ((w == 0) & (col == 0))
+        bcol = jnp.where(split_col, BIG, 0.0)
+        bias = jnp.where(((lane == C + 1) & kcol) | ((lane == C + 2) & ~kcol), bcol, 0.0)
+        if near:
+            rows = pl.ds(8 + ry * 8, 8)
+        else:
+            rows = pl.ds(ry * 24, 8)
+            bias = bias + jnp.where(lane == C, jnp.where(split_row, BIG, 0.0), 0.0)
+        q = (qe[pl.ds(ry * 8, 8), cols].astype(F32) + qpat).astype(BF16).reshape(8 * WIN, L)
+        kk = (ke[rows, cols].astype(F32) + bias).astype(BF16).reshape(8 * WIN, L)
+        vv = ve[rows, cols].reshape(8 * WIN, L)
+        return attend_part(q, kk, vv, HEADS)
+
+    def shifted_near(k, count, width, first, stride):
+        def step(i, carry):
+            ry = i // width
+            w = first + stride * (i - ry * width)
+            keep_part(pl.ds(ry * 5 + w, 1), shifted_part(k, ry, w, True))
+            return carry
+
+        lax.fori_loop(0, count, step, 0)
+
+    def shifted_far(k):
         def step(i, carry):
             ry = i // 5
             w = i - ry * 5
             cols = pl.ds(pl.multiple_of(w * WIN, WIN), WIN)
-            split_row = ((ry == 1) & (row == ROWS - 1)) | ((ry == 0) & (row == 0))
-            split_col = ((w == 4) & (col == COLS - 1)) | ((w == 0) & (col == 0))
-            brow = jnp.where(split_row, BIG, 0.0)
-            bcol = jnp.where(split_col, BIG, 0.0)
-            other = jnp.where(ry == 0, 0.0, 1.0)
-            krf = jnp.where(krow, 1.0, 0.0)
-            differs = krf * other + (1.0 - krf) * (1.0 - other)
-            bias = jnp.where(lane == C, differs * brow, 0.0) + jnp.where(
-                ((lane == C + 1) & kcol) | ((lane == C + 2) & ~kcol), bcol, 0.0
-            )
-            q = (qe[pl.ds(ry * 8, 8), cols].astype(F32) + qpat).astype(BF16)
-            kk = (ke[pl.ds(ry * WIN, WIN), cols].astype(F32) + bias).astype(BF16)
-            vv = ve[pl.ds(ry * WIN, WIN), cols]
-            o = attend(
-                q.reshape(8 * WIN, L), kk.reshape(WIN * WIN, L), vv.reshape(WIN * WIN, L), HEADS
-            )
+            o = merge_parts(kept_part(pl.ds(i, 1)), shifted_part(k, ry, w, False))
             att[pl.ds(ry * 8, 8), cols] = dot(o, wp[k]).reshape(8, WIN, L)
             return carry
 
         return step
 
-    def cross_window(k):
+    def cross_part(k, w, rows):
         lane = iota((1, 1, L), 2)
         qpat = jnp.where(lane == C, 1.0, 0.0)
         kcol = iota((1, 32, 1), 1)
         bias = jnp.where((lane == C) & ((kcol < 4) | (kcol >= 28)), BIG, 0.0)
-
+        cols = pl.ds(pl.multiple_of(w * WIN, WIN), WIN)
+        wide = pl.ds(pl.multiple_of(w * WIN, WIN), 32)
+        q = (qs[:, cols].astype(F32) + qpat).astype(BF16).reshape(WIN * WIN, L)
+        kk = jnp.concatenate([ke[r, wide] for r in rows], axis=0)
+        vv = jnp.concatenate([ve[r, wide] for r in rows], axis=0)
+        n = kk.shape[0] * 32
+        kk = (kk.astype(F32) + bias).astype(BF16).reshape(n, L)
+        return attend_part(q, kk, vv.reshape(n, L), 2)
+
+    def cross_near(k, first, stride):
+        def step(i, carry):
+            w = first + stride * i
+            keep_part(pl.ds(2 * w, 2), cross_part(k, w, (pl.ds(8, 16),)))
+            return carry
+
+        lax.fori_loop(0, 2, step, 0)
+
+    def cross_far(k):
         def step(w, carry):
             cols = pl.ds(pl.multiple_of(w * WIN, WIN), WIN)
-            wide = pl.ds(pl.multiple_of(w * WIN, WIN), 32)
-            q = (qs[:, cols].astype(F32) + qpat).astype(BF16).reshape(WIN * WIN, L)
-            kk = (ke[pl.ds(4, 24), wide].astype(F32) + bias).astype(BF16).reshape(24 * 32, L)
-            vv = ve[pl.ds(4, 24), wide].reshape(24 * 32, L)
-            o = attend(q, kk, vv, 2)
+            far = cross_part(k, w, (pl.ds(4, 4), pl.ds(24, 4)))
+            o = merge_parts(kept_part(pl.ds(2 * w, 2)), far)
             att[:, cols] = dot(o, wp[k]).reshape(WIN, WIN, L)
             return carry
 
@@ -431,92 +500,121 @@
         z = jnp.sum(gu[k] * squeezed, axis=0, keepdims=True)
         return 1.0 / (1.0 + jnp.exp(-z))
 
-    def feed_forward(k, scale, offset):
-        chunk = 8
-
-        def step(i, carry):
-            rows = pl.ds(i * chunk, chunk)
+    def feed_forward(k, scale, offset, spans):
+        parts = []
+        for at, n in spans:
+            rows = slice(at, at + n)
             x = st[rows] + att[rows, offset : offset + W]
             if scale is not None:
                 x = x + ex[rows] * scale.reshape(1, 1, L)
-            u = layer_norm(x).astype(BF16).reshape(chunk * W, L)
-            h = gelu(dot(u, m1[k])).astype(BF16)
-            st[rows] = x + dot(h, m2[k]).reshape(chunk, W, L)
-            return carry
-
-        lax.fori_loop(0, H // chunk, step, 0)
+            parts.append(x)
+        x = jnp.concatenate(parts, axis=0)
+        u = layer_norm(x).astype(BF16).reshape(8 * W, L)
+        h = gelu(dot(u, m1[k])).astype(BF16)
+        y = x + dot(h, m2[k]).reshape(8, W, L)
+        done = 0
+        for at, n in spans:
+            part = y[done : done + n]
+            done += n
+            if k < 3:
+                st[at : at + n] = part
+                normalize(k + 1, part, pl.ds(at, n))
+            else:
+                out[at : at + n] = part[:, :, :C].astype(out.dtype)
+
+    def block_end(k, scale, offset, g):
+        feed_forward(k, scale, offset, ((0, 4), (12, 4)))
+        rows = send_rows(g) if k < 3 else None
+        feed_forward(k, scale, offset, ((4, 8),))
+        sides = send_sides(g) if k < 3 else None
+        return rows, sides
 
     st[...] = jnp.zeros_like(st)
     st[:, :, :C] = tok[...].astype(F32)
 
-    normalize(0)
+    for i in range(2):
+        normalize(0, st[8 * i : 8 * i + 8], pl.ds(8 * i, 8))
     pl.semaphore_wait(barrier, len(peers))
-    halos = send(0)
+    rows, sides = send_rows(0), send_sides(0)
     finish(loads)
     prepare_attention(0)
     prepare_conv(0)
-    project(0, un, ((0, qs, 0), (1, ks, 0), (2, vs, 0)), 0, H, W, 8)
+    prepare_mlp(0)
+    prepare_attention(1)
+    project_plain(0, (qs, ks, vs))
     lax.fori_loop(0, 1, plain_window(0), 0)
-    finish(halos)
-    receive(0, ue, None)
+    finish(rows)
+    finish(sides)
+    receive_rows(0, ue, None)
+    receive_sides(0, ue, None)
     conv_in(0)
     ara[0, 0] = conv_out(0)
     copies = stage_a(0)
     start(copies)
     lax.fori_loop(1, 4, plain_window(0), 0)
     copies = between(0, copies)
-    for k in range(4):
-        prepare_mlp(k)
-    for k in range(1, 4):
-        prepare_attention(k)
-    for k in range(1, 3):
-        prepare_conv(k)
-    feed_forward(0, gate(0, copies), 0)
-
-    normalize(1)
-    halos = send(1)
-    more = send(2)
-    finish(halos)
-    receive(1, ue, ua)
+    prepare_conv(1)
+    prepare_mlp(1)
+    prepare_attention(2)
+    prepare_conv(2)
+    rows, sides = block_end(0, gate(0, copies), 0, 1)
+
+    more = send_rows(2)
+    project_inner(1, ua, ((0, qe, 8), (1, ke, 0), (2, ve, 0)))
+    shifted_near(1, 6, 3, 1, 1)
+    finish(sides)
+    receive_sides(1, ue, ua)
+    project_sides(1, ua, ((0, qe, 8), (1, ke, 0), (2, ve, 0)))
+    finish(rows)
+    receive_rows(1, ue, ua)
     conv_in(1)
     ara[1, 0] = conv_out(1)
     copies = stage_a(1)
     start(copies)
-    project(1, ua, ((0, qe, 8), (1, ke, 0), (2, ve, 0)), 8, H, E, 4)
+    shifted_near(1, 4, 2, 0, 4)
+    finish(more)
+    receive_rows(2, None, ua)
+    project_rows(1, ua, 8)
     copies = between(1, copies)
-    finish(more)
-    receive(2, None, ua)
-    project(1, ua, ((1, ke, 0), (2, ve, 0)), 0, 8, E, 4)
-    project(1, ua, ((1, ke, 0), (2, ve, 0)), 24, 8, E, 4)
-    lax.fori_loop(0, 10, shifted_window(1), 0)
-    feed_forward(1, gate(1, copies), 8)
-
-    normalize(2)
-    halos = send(3)
-    project(2, un, ((0, qs, 0), (1, ks, 0), (2, vs, 0)), 0, H, W, 8)
+    lax.fori_loop(0, 10, shifted_far(1), 0)
+    rows, sides = block_end(1, gate(1, copies), 8, 3)
+
+    project_plain(2, (qs, ks, vs))
     lax.fori_loop(0, 2, plain_window(2), 0)
-    finish(halos)
-    receive(3, ue, None)
+    finish(sides)
+    finish(rows)
+    receive_sides(3, ue, None)
+    receive_rows(3, ue, None)
     conv_in(2)
     ara[2, 0] = conv_out(2)
     copies = stage_a(2)
     start(copies)
     lax.fori_loop(2, 4, plain_window(2), 0)
     copies = between(2, copies)
-    feed_forward(2, gate(2, copies), 0)
-
-    normalize(3)
-    halos = send(4)
-    project(3, un, ((0, qs, 0),), 0, H, W, 8)
-    finish(halos)
-    receive(4, ue, None)
-    project(3, ue, ((1, ke, 0), (2, ve, 0)), 4, 24, E, 6)
-    lax.fori_loop(0, 4, cross_window(3), 0)
-    feed_forward(3, None, 0)
-    out[...] = st[:, :, :C].astype(BF16)
-
-
-def local(*args):
+    prepare_mlp(2)
+    prepare_attention(3)
+    prepare_mlp(3)
+    rows, sides = block_end(2, gate(2, copies), 0, 4)
+
+    project_plain(3, (qs,))
+    project_inner(3, ue, ((1, ke, 0), (2, ve, 0)))
+    cross_near(3, 1, 1)
+    finish(sides)
+    receive_sides(4, ue, None)
+    project_sides(3, ue, ((1, ke, 0), (2, ve, 0)))
+    cross_near(3, 0, 3)
+    finish(rows)
+    receive_rows(4, ue, None)
+    project_rows(3, ue, 4)
+    lax.fori_loop(0, 4, cross_far(3), 0)
+    block_end(3, None, 0, None)
+
+
+def local(tok, qkv, proj, squeeze, expand, down, up_, mlp_in, mlp_out, oqkv, oproj):
+    args = (
+        tok, qkv, proj, squeeze.transpose(0, 1, 3, 2), expand, down.transpose(0, 2, 1), up_,
+        mlp_in.transpose(1, 0, 2), mlp_out.transpose(2, 0, 1), oqkv, oproj,
+    )
     vmem = pl.BlockSpec(memory_space=pltpu.VMEM)
     hbm = pl.BlockSpec(memory_space=pltpu.HBM)
     scratch = [pltpu.VMEM(a.shape, a.dtype) for a in args[1:]]
@@ -529,7 +627,10 @@
         pltpu.VMEM((3, 8, L), F32),
         pltpu.VMEM((4, L, HL), BF16),
         pltpu.VMEM((4, HL, L), BF16),
-        pltpu.VMEM((L, 128), F32),
+        pltpu.VMEM((L, HL), BF16),
+        pltpu.VMEM((10, 128, L), F32),
+        pltpu.VMEM((10, 128, L), F32),
+        pltpu.VMEM((10, 128, L), F32),
         pltpu.VMEM((H, W, L), F32),
         pltpu.VMEM((H, W, L), BF16),
         pltpu.VMEM((32, E, L), BF16),

time: 103 us -> 90.9 us (0.88); the launches traced: 101 us -> 90.7 us
  local copies, waits for them, and re-layouts: 8.76 us -> 1.88 us
  Pallas kernels: 92.7 us -> 88.8 us
    unnamed x9 -> x1, local copies, waits for them, and re-layouts: 8.76 us -> 1.88 us
    pallas_call x1, Pallas kernels: 92.7 us -> 88.8 us  [local(): pl.pallas_call(kernel, out_shape=jax.ShapeDtypeStruct((H, W, C), BF16), i...]
where the time goes in v2:
time: 90.9 us; the launch traced here: 90.7 us
  Pallas kernels  88.8 us (98%)
  local copies, waits for them, and re-layouts  1.88 us (2%)
    pallas_call x1, Pallas kernels, local(): pl.pallas_call(kernel, out_shape=jax.ShapeDtypeStruct((H, W, C), BF16), i...  88.8 us
    unnamed x1, local copies, waits for them, and re-layouts  1.88 us

profile of v2, /device:TPU:0, one launch (start us, length us, event | category | flops | bytes accessed | tf_op | source)
XLA Modules:
  0.0 90.7 jit_solution(13172338717557353473)
XLA Ops:
  0.0 88.8 %blocks.1 = bf16[16,64,180]{2,1,0:T(8,128)(2,1)} custom-call(bf16[16,64,180]{2,1,0:T(8,128)(2,1)} %refs_0_.1, bf16[3,180,540]{2,1,0:T(8,128)(2,1)} %refs_1_.1, bf16[3,180,180]{2,1,0:T(8,128)(2,1)} %refs_2_.1, bf16[3,9,60,180]{3,2,1,0:T(8,128)(2,1)} %bitcast.4, bf16[3,9,60,180]{3,2,1,0:T(8,128)(2,1)} %refs_4_.1, bf16[3,6,180]{2,1,0:T(8,128)(2,1)} %bitcast.7, ...), custom_call_target="tpu_custom_call" | custom-call | tf_op jit(solution)/shard_map/blocks/pallas_call | solution.py:656
  88.8 1.9 %copy.13 = bf16[16,64,180]{2,1,0:T(8,128)(2,1)} copy(bf16[16,64,180]{2,1,0:T(8,128)(2,1)} %blocks.1) | data formatting | bytes 737280

commit v3 on v2

--- a/solution.py
+++ b/solution.py
@@ -130,10 +130,10 @@
         tok, qkv_h, proj_h, sq_h, ex_h, gd_h, gu_h, m1_h, m2_h, oqkv_h, oproj_h, out,
         rqkv, rproj, rsq, rex, rgd, rgu, rm1, rm2, roqkv, roproj,
         wqkv, wp, w1, w2, gd, gu, m1, m2, tmp, pn, pm, pd,
-        st, un, ue, ua, qs, ks, vs, qe, ke, ve, att, ex, h32, ara, arb,
+        st, un, ue, ua, qs, ks, vs, qe, ke, ve, oe, att, ex, h32, arf,
     ) = refs[:49]
     bufs = refs[49 : 49 + 6 * len(GROUPS)]
-    wsem, hs, hr, asend, arecv, bsend, brecv = refs[49 + 6 * len(GROUPS) :]
+    wsem, hs, hr, asend, arecv, ready = refs[49 + 6 * len(GROUPS) :]
     row_s, row_r, col_s, col_r, cor_s, cor_r = (bufs[i :: 6] for i in range(6))
     row = lax.axis_index("row")
     col = lax.axis_index("col")
@@ -141,11 +141,28 @@
     left, right = lax.rem(col + COLS - 1, COLS), lax.rem(col + 1, COLS)
 
     barrier = pltpu.get_barrier_semaphore()
-    peers = [(lax.rem(row + d, ROWS), col) for d in range(1, ROWS)]
-    peers += [(row, lax.rem(col + d, COLS)) for d in range(1, COLS)]
+    others = ROWS * COLS - 1
+
+    def peer(dr, dc):
+        return lax.rem(row + dr, ROWS), lax.rem(col + dc, COLS)
+
+    def for_others(act):
+        for dr in (4, 3, 5, 2, 6, 1, 7, 0):
+
+            def step(i, carry, dr=dr):
+                act(dr, lax.rem(i + COLS // 2, COLS))
+                return carry
+
+            if dr:
+                lax.fori_loop(0, COLS, step, 0, unroll=4)
+            else:
+                lax.fori_loop(0, COLS // 2, step, 0)
+                lax.fori_loop(COLS // 2 + 1, COLS, step, 0)
+
+    peers = [peer(d, 0) for d in range(1, ROWS)] + [peer(0, d) for d in range(1, COLS)]
     peers += [(up, left), (up, right), (down, left), (down, right)]
-    for peer in peers:
-        pl.semaphore_signal(barrier, inc=1, device_id=peer, device_id_type=MESH)
+    for p in peers:
+        pl.semaphore_signal(barrier, inc=1, device_id=p, device_id_type=MESH)
 
     loads = [
         pltpu.make_async_copy(s, d, wsem.at[i])
@@ -236,9 +253,10 @@
         pack(fold(top[:, W - 8 : W]), cor_s[g].at[1])
         pack(fold(low[:, 0:8]), cor_s[g].at[2])
         pack(fold(low[:, W - 8 : W]), cor_s[g].at[3])
-        rows = copies_of(g, (0, 1, 4, 5, 6, 7))
-        start(rows)
-        return rows
+        low_half, top_half = copies_of(g, (1, 6, 7)), copies_of(g, (0, 4, 5))
+        start(low_half)
+        start(top_half)
+        return low_half, top_half
 
     def send_sides(g):
         pack(fold(un[:, 0:16].astype(F32)[:, 0:8]), col_s[g].at[0])
@@ -252,10 +270,12 @@
     yes_left = jnp.where(col > 0, 1.0, 0.0)
     yes_right = jnp.where(col < COLS - 1, 1.0, 0.0)
 
-    def receive_rows(g, masked, whole):
+    def receive_rows(g, masked, whole, sides=(1, 0)):
         d0, n, _ = GROUPS[g]
         m = n // 2
         for which, lc, rc, at, keep in ((1, 3, 2, 8 - d0 - n, yes_up), (0, 1, 0, 24 + d0, yes_down)):
+            if which not in sides:
+                continue
             mid = unpack(row_r[g].at[which], n)
             lcorner = unfold(unpack(cor_r[g].at[lc], m))
             rcorner = unfold(unpack(cor_r[g].at[rc], m))
@@ -320,8 +340,8 @@
             dst[8 - base : 24 - base, 0:16] = y[:, 0:16]
             dst[8 - base : 24 - base, 64:80] = y[:, 16:32]
 
-    def project_rows(k, src, n):
-        for at in (8 - n, 24):
+    def project_rows(k, src, n, sides=(1, 0)):
+        for at in [(24, 8 - n)[side] for side in sides]:
             x = src[at : at + n]
             for which, dst in ((1, ke), (2, ve)):
                 dst[at : at + n] = project(k, which, x)
@@ -339,62 +359,38 @@
 
         return step
 
-    def keep_part(at, part):
-        for ref, value in zip((pn, pm, pd), part):
-            ref[at] = value.reshape(at.size, 128, L)
-
-    def kept_part(at):
-        return tuple(ref[at].reshape(at.size * 128, L) for ref in (pn, pm, pd))
-
-    def shifted_part(k, ry, w, near):
+    def shifted_windows(k, ry):
         lane = iota((1, 1, L), 2)
         qcol = iota((8, WIN, 1), 1) >= 8
         qpat = jnp.where(lane == C, 1.0, 0.0) + jnp.where(
             ((lane == C + 1) & ~qcol) | ((lane == C + 2) & qcol), 1.0, 0.0
         )
-        kcol = iota((8, WIN, 1), 1) >= 8
-        cols = pl.ds(pl.multiple_of(w * WIN, WIN), WIN)
-        split_row = ((ry == 1) & (row == ROWS - 1)) | ((ry == 0) & (row == 0))
-        split_col = ((w == 4) & (col == COLS - 1)) | ((w == 0) & (col == 0))
-        bcol = jnp.where(split_col, BIG, 0.0)
-        bias = jnp.where(((lane == C + 1) & kcol) | ((lane == C + 2) & ~kcol), bcol, 0.0)
-        if near:
-            rows = pl.ds(8 + ry * 8, 8)
-        else:
-            rows = pl.ds(ry * 24, 8)
-            bias = bias + jnp.where(lane == C, jnp.where(split_row, BIG, 0.0), 0.0)
-        q = (qe[pl.ds(ry * 8, 8), cols].astype(F32) + qpat).astype(BF16).reshape(8 * WIN, L)
-        kk = (ke[rows, cols].astype(F32) + bias).astype(BF16).reshape(8 * WIN, L)
-        vv = ve[rows, cols].reshape(8 * WIN, L)
-        return attend_part(q, kk, vv, HEADS)
-
-    def shifted_near(k, count, width, first, stride):
-        def step(i, carry):
-            ry = i // width
-            w = first + stride * (i - ry * width)
-            keep_part(pl.ds(ry * 5 + w, 1), shifted_part(k, ry, w, True))
-            return carry
-
-        lax.fori_loop(0, count, step, 0)
-
-    def shifted_far(k):
-        def step(i, carry):
-            ry = i // 5
-            w = i - ry * 5
-            cols = pl.ds(pl.multiple_of(w * WIN, WIN), WIN)
-            o = merge_parts(kept_part(pl.ds(i, 1)), shifted_part(k, ry, w, False))
-            att[pl.ds(ry * 8, 8), cols] = dot(o, wp[k]).reshape(8, WIN, L)
-            return carry
-
-        return step
-
-    def cross_part(k, w, rows):
+        krow = iota((WIN, WIN, 1), 0) >= 8
+        kcol = iota((WIN, WIN, 1), 1) >= 8
+        differs = krow if ry == 1 else ~krow
+        brow = jnp.where(row == (ROWS - 1 if ry == 1 else 0), BIG, 0.0)
+        rbias = jnp.where((lane == C) & differs, brow, 0.0)
+        for w in range(5):
+            cols = slice(w * WIN, (w + 1) * WIN)
+            bias = rbias
+            if w in (0, 4):
+                bcol = jnp.where(col == (COLS - 1 if w == 4 else 0), BIG, 0.0)
+                bias = bias + jnp.where(((lane == C + 1) & kcol) | ((lane == C + 2) & ~kcol), bcol, 0.0)
+            q = (qe[8 * ry : 8 * ry + 8, cols].astype(F32) + qpat).astype(BF16)
+            kk = (ke[WIN * ry : WIN * ry + WIN, cols].astype(F32) + bias).astype(BF16)
+            vv = ve[WIN * ry : WIN * ry + WIN, cols]
+            o = attend(q.reshape(8 * WIN, L), kk.reshape(WIN * WIN, L), vv.reshape(WIN * WIN, L), HEADS)
+            oe[8 * ry : 8 * ry + 8, cols] = o.reshape(8, WIN, L)
+        o = oe[8 * ry : 8 * ry + 8].reshape(8 * E, L)
+        att[8 * ry : 8 * ry + 8] = dot(o, wp[k]).reshape(8, E, L)
+
+    def cross_part(w, rows):
         lane = iota((1, 1, L), 2)
         qpat = jnp.where(lane == C, 1.0, 0.0)
         kcol = iota((1, 32, 1), 1)
         bias = jnp.where((lane == C) & ((kcol < 4) | (kcol >= 28)), BIG, 0.0)
-        cols = pl.ds(pl.multiple_of(w * WIN, WIN), WIN)
-        wide = pl.ds(pl.multiple_of(w * WIN, WIN), 32)
+        cols = slice(w * WIN, (w + 1) * WIN)
+        wide = slice(w * WIN, w * WIN + 32)
         q = (qs[:, cols].astype(F32) + qpat).astype(BF16).reshape(WIN * WIN, L)
         kk = jnp.concatenate([ke[r, wide] for r in rows], axis=0)
         vv = jnp.concatenate([ve[r, wide] for r in rows], axis=0)
@@ -402,23 +398,19 @@
         kk = (kk.astype(F32) + bias).astype(BF16).reshape(n, L)
         return attend_part(q, kk, vv.reshape(n, L), 2)
 
-    def cross_near(k, first, stride):
-        def step(i, carry):
-            w = first + stride * i
-            keep_part(pl.ds(2 * w, 2), cross_part(k, w, (pl.ds(8, 16),)))
-            return carry
-
-        lax.fori_loop(0, 2, step, 0)
+    def cross_near(windows):
+        for w in windows:
+            part = cross_part(w, (slice(8, 24),))
+            for ref, value in zip((pn, pm, pd), part):
+                ref[w] = value
 
     def cross_far(k):
-        def step(w, carry):
-            cols = pl.ds(pl.multiple_of(w * WIN, WIN), WIN)
-            far = cross_part(k, w, (pl.ds(4, 4), pl.ds(24, 4)))
-            o = merge_parts(kept_part(pl.ds(2 * w, 2)), far)
-            att[:, cols] = dot(o, wp[k]).reshape(WIN, WIN, L)
-            return carry
-
-        return step
+        for w in range(4):
+            far = cross_part(w, (slice(4, 8), slice(24, 28)))
+            o = merge_parts(tuple(ref[w] for ref in (pn, pm, pd)), far)
+            oe[:, w * WIN : (w + 1) * WIN] = o.reshape(WIN, WIN, L)
+        o = oe[:, 0:W].reshape(H * W, L)
+        att[:, 0:W] = dot(o, wp[k]).reshape(H, W, L)
 
 
     def conv_in(k):
@@ -443,15 +435,16 @@
             g = gelu(s)
             at = hrow + i * chunk
             ok = (at >= rlow) & (at < rhigh) & (hcol >= low) & (hcol < high) & (lane < 60)
-            h32[pl.ds(i * chunk, chunk)] = jnp.where(ok, g, 0.0)
+            h32[pl.ds(i * chunk, chunk)] = jnp.where(ok, g, 0.0).astype(BF16).astype(F32)
             return carry
 
-        lax.fori_loop(0, 18 // chunk, step, 0)
+        for i in range(18 // chunk):
+            step(i, 0)
 
     def conv_out(k):
         chunk = 8
 
-        def step(i, total):
+        def step(i, carry):
             lead = h32[pl.ds(i * chunk, chunk)]
             mid = h32[pl.ds(i * chunk + 1, chunk)]
             tail = h32[pl.ds(i * chunk + 2, chunk)]
@@ -462,38 +455,64 @@
             r2 = dot(x, w2[k, 2]).reshape(chunk, E, L)
             y = (pltpu.roll(r0, 1, 1) + r1 + pltpu.roll(r2, E - 1, 1))[:, 8:72]
             ex[pl.ds(i * chunk, chunk)] = y
-            return total + jnp.sum(jnp.sum(y, axis=0), axis=0, keepdims=True)
-
-        return lax.fori_loop(0, H // chunk, step, jnp.zeros((1, L), F32))
-
-
-    def stage_a(k):
-        return [
-            remote(ara.at[k, 0], ara.at[k, d], asend.at[k, d], arecv.at[k, d], (lax.rem(row + d, ROWS), col))
-            for d in range(1, ROWS)
-        ]
-
-    def stage_b(k):
-        return [
-            remote(arb.at[k, 0], arb.at[k, d], bsend.at[k, d], brecv.at[k, d], (row, lax.rem(col + d, COLS)))
-            for d in range(1, COLS)
-        ]
-
-    def between(k, copies):
-        finish(copies)
-        s = ara[k, 0]
-        for d in range(1, ROWS):
-            s = s + ara[k, d]
-        arb[k, 0] = s
-        nxt = stage_b(k)
-        start(nxt)
-        return nxt
-
-    def gate(k, copies):
-        finish(copies)
-        s = arb[k, 0]
-        for d in range(1, COLS):
-            s = s + arb[k, d]
+            return carry
+
+        lax.fori_loop(0, H // chunk, step, 0)
+
+
+    is_top, is_low = 1.0 - yes_up, 1.0 - yes_down
+    is_left, is_right = 1.0 - yes_left, 1.0 - yes_right
+
+    def expanded_sum(k):
+        def over(x):
+            return jnp.sum(jnp.sum(x, axis=0), axis=0, keepdims=True)
+
+        every = over(h32[1:17, 8:72])
+        top, low = over(h32[1:2, 8:72]) * is_top, over(h32[16:17, 8:72]) * is_low
+        lead, tail = h32[1:17, 8:16][:, 0:1], h32[1:17, 64:72][:, 7:8]
+        left_, right_ = over(lead) * is_left, over(tail) * is_right
+        rows_out = (low, None, top)
+        cols_out = (right_, None, left_)
+        corner = {
+            (0, 0): tail[15] * (is_low * is_right),
+            (0, 2): lead[15] * (is_low * is_left),
+            (2, 0): tail[0] * (is_top * is_right),
+            (2, 2): lead[0] * (is_top * is_left),
+        }
+        total = None
+        for b in range(3):
+            s = []
+            for a in range(3):
+                v = every
+                if rows_out[a] is not None:
+                    v = v - rows_out[a]
+                if cols_out[b] is not None:
+                    v = v - cols_out[b]
+                if (a, b) in corner:
+                    v = v + corner[a, b]
+                s.append(v)
+            v = jnp.concatenate([s[0] + pltpu.roll(jnp.broadcast_to(s[1], (8, 128)), 64, 1)[0:1], s[2]], axis=1)
+            first = v.astype(BF16).astype(F32)
+            second = (v - first).astype(BF16).astype(F32)
+            third = v - first - second
+            x = jnp.concatenate([first, second, third, jnp.zeros((5, L), F32)], axis=0).astype(BF16)
+            y = jnp.sum(dot(x, w2[k, b]), axis=0, keepdims=True)
+            total = y if total is None else total + y
+        return total
+
+    def spread(k, part):
+        arf[k, 0] = part
+
+        def one(dr, dc):
+            slot = dr * COLS + dc
+            remote(arf.at[k, 0], arf.at[k, slot], asend.at[k], arecv.at[k], peer(dr, dc)).start()
+
+        for_others(one)
+
+    def gate(k):
+        rest = arf.at[k, pl.ds(1, others)]
+        remote(rest, rest, asend.at[k], arecv.at[k], (row, col)).wait()
+        s = jnp.sum(arf[k], axis=0)
         pooled = s * (1.0 / (ROWS * COLS * H * W))
         squeezed = jnp.sum(gd[k] * pooled, axis=-1, keepdims=True)
         squeezed = jnp.maximum(squeezed, 0.0)
@@ -536,77 +555,73 @@
         normalize(0, st[8 * i : 8 * i + 8], pl.ds(8 * i, 8))
     pl.semaphore_wait(barrier, len(peers))
     rows, sides = send_rows(0), send_sides(0)
+    for d in range(1, COLS):
+        pl.semaphore_signal(ready, inc=1, device_id=peer(0, d), device_id_type=MESH)
     finish(loads)
     prepare_attention(0)
     prepare_conv(0)
+    project_plain(0, (qs, ks, vs))
     prepare_mlp(0)
     prepare_attention(1)
-    project_plain(0, (qs, ks, vs))
-    lax.fori_loop(0, 1, plain_window(0), 0)
-    finish(rows)
-    finish(sides)
+    prepare_conv(1)
+    finish(sides + rows[0] + rows[1])
+    receive_sides(0, ue, None)
     receive_rows(0, ue, None)
-    receive_sides(0, ue, None)
     conv_in(0)
-    ara[0, 0] = conv_out(0)
-    copies = stage_a(0)
-    start(copies)
-    lax.fori_loop(1, 4, plain_window(0), 0)
-    copies = between(0, copies)
-    prepare_conv(1)
+    part = expanded_sum(0)
+    pl.semaphore_wait(ready, COLS - 1)
+    spread(0, part)
+    conv_out(0)
+    lax.fori_loop(0, 4, plain_window(0), 0)
     prepare_mlp(1)
     prepare_attention(2)
     prepare_conv(2)
-    rows, sides = block_end(0, gate(0, copies), 0, 1)
+    prepare_mlp(2)
+    rows, sides = block_end(0, gate(0), 0, 1)
 
     more = send_rows(2)
     project_inner(1, ua, ((0, qe, 8), (1, ke, 0), (2, ve, 0)))
-    shifted_near(1, 6, 3, 1, 1)
     finish(sides)
     receive_sides(1, ue, ua)
     project_sides(1, ua, ((0, qe, 8), (1, ke, 0), (2, ve, 0)))
-    finish(rows)
+    finish(rows[0] + rows[1])
     receive_rows(1, ue, ua)
     conv_in(1)
-    ara[1, 0] = conv_out(1)
-    copies = stage_a(1)
-    start(copies)
-    shifted_near(1, 4, 2, 0, 4)
-    finish(more)
-    receive_rows(2, None, ua)
-    project_rows(1, ua, 8)
-    copies = between(1, copies)
-    lax.fori_loop(0, 10, shifted_far(1), 0)
-    rows, sides = block_end(1, gate(1, copies), 8, 3)
+    spread(1, expanded_sum(1))
+    conv_out(1)
+    finish(more[0])
+    receive_rows(2, None, ua, (1,))
+    project_rows(1, ua, 8, (1,))
+    shifted_windows(1, 0)
+    finish(more[1])
+    receive_rows(2, None, ua, (0,))
+    project_rows(1, ua, 8, (0,))
+    shifted_windows(1, 1)
+    rows, sides = block_end(1, gate(1), 8, 3)
 
     project_plain(2, (qs, ks, vs))
-    lax.fori_loop(0, 2, plain_window(2), 0)
-    finish(sides)
-    finish(rows)
+    prepare_attention(3)
+    prepare_mlp(3)
+    finish(sides + rows[0] + rows[1])
     receive_sides(3, ue, None)
     receive_rows(3, ue, None)
     conv_in(2)
-    ara[2, 0] = conv_out(2)
-    copies = stage_a(2)
-    start(copies)
-    lax.fori_loop(2, 4, plain_window(2), 0)
-    copies = between(2, copies)
-    prepare_mlp(2)
-    prepare_attention(3)
-    prepare_mlp(3)
-    rows, sides = block_end(2, gate(2, copies), 0, 4)
+    spread(2, expanded_sum(2))
+    conv_out(2)
+    lax.fori_loop(0, 4, plain_window(2), 0)
+    rows, sides = block_end(2, gate(2), 0, 4)
 
     project_plain(3, (qs,))
     project_inner(3, ue, ((1, ke, 0), (2, ve, 0)))
-    cross_near(3, 1, 1)
+    cross_near((1, 2))
     finish(sides)
     receive_sides(4, ue, None)
     project_sides(3, ue, ((1, ke, 0), (2, ve, 0)))
-    cross_near(3, 0, 3)
-    finish(rows)
+    cross_near((0, 3))
+    finish(rows[0] + rows[1])
     receive_rows(4, ue, None)
     project_rows(3, ue, 4)
-    lax.fori_loop(0, 4, cross_far(3), 0)
+    cross_far(3)
     block_end(3, None, 0, None)
 
 
@@ -628,9 +643,9 @@
         pltpu.VMEM((4, L, HL), BF16),
         pltpu.VMEM((4, HL, L), BF16),
         pltpu.VMEM((L, HL), BF16),
-        pltpu.VMEM((10, 128, L), F32),
-        pltpu.VMEM((10, 128, L), F32),
-        pltpu.VMEM((10, 128, L), F32),
+        pltpu.VMEM((4, WIN * WIN, L), F32),
+        pltpu.VMEM((4, WIN * WIN, L), F32),
+        pltpu.VMEM((4, WIN * WIN, L), F32),
         pltpu.VMEM((H, W, L), F32),
         pltpu.VMEM((H, W, L), BF16),
         pltpu.VMEM((32, E, L), BF16),
@@ -641,21 +656,21 @@
         pltpu.VMEM((H, E, L), BF16),
         pltpu.VMEM((32, E, L), BF16),
         pltpu.VMEM((32, E, L), BF16),
+        pltpu.VMEM((H, E, L), BF16),
         pltpu.VMEM((H, E, L), F32),
         pltpu.VMEM((H, W, L), F32),
         pltpu.VMEM((18, E, 128), F32),
-        pltpu.VMEM((3, ROWS, 1, L), F32),
-        pltpu.VMEM((3, COLS, 1, L), F32),
+        pltpu.VMEM((3, ROWS * COLS, 1, L), F32),
     ]
     for _, n, _ in GROUPS:
         for shape in ((2, packed(n), W, 128), (2, packed(8), 16, 128), (4, packed(n // 2), 16, 128)):
             scratch += [pltpu.VMEM(shape, BF16)] * 2
     dma = pltpu.SemaphoreType.DMA
     scratch += [dma((10,)), dma((len(GROUPS), 8)), dma((len(GROUPS), 8))]
-    scratch += [dma((3, ROWS)), dma((3, ROWS)), dma((3, COLS)), dma((3, COLS))]
+    scratch += [dma((3,)), dma((3,)), pltpu.SemaphoreType.REGULAR]
     return pl.pallas_call(
         kernel,
-        out_shape=jax.ShapeDtypeStruct((H, W, C), BF16),
+        out_shape=jax.ShapeDtypeStruct((H, W, C), F32),
         in_specs=[vmem] + [hbm] * 10,
         out_specs=vmem,
         scratch_shapes=scratch,
@@ -663,7 +678,7 @@
             collective_id=0, has_side_effects=True, vmem_limit_bytes=60 * 1024 * 1024
         ),
         name="blocks",
-    )(*args)
+    )(*args).astype(BF16)
 
 
 def solution(mesh):

time: 90.9 us -> 78.6 us (0.86)
  Pallas kernels: 88.8 us -> 76.3 us
  other arithmetic: 0 us -> 2.09 us
  local copies, waits for them, and re-layouts: 1.88 us -> 0 us
    pallas_call x1, Pallas kernels: 88.8 us -> 76.3 us  [local(): pl.pallas_call(kernel, out_shape=jax.ShapeDtypeStruct((H, W, C), F32), in...]
    convert_element_type x0 -> x1, other arithmetic: none -> 2.09 us  [local(): return pl.pallas_call(kernel, out_shape=jax.ShapeDtypeStruct((H, W, C), F...]
    unnamed x1 -> x0, local copies, waits for them, and re-layouts: 1.88 us -> none
where the time goes in v3:
time: 78.6 us; the launch traced here: 78.4 us
  Pallas kernels  76.3 us (97%)
  other arithmetic  2.09 us (3%)
    pallas_call x1, Pallas kernels, local(): pl.pallas_call(kernel, out_shape=jax.ShapeDtypeStruct((H, W, C), F32), in...  76.3 us
    convert_element_type x1, other arithmetic, local(): return pl.pallas_call(kernel, out_shape=jax.ShapeDtypeStruct((H, W, C), F...  2.09 us

profile of v3, /device:TPU:0, one launch (start us, length us, event | category | flops | bytes accessed | tf_op | source)
XLA Modules:
  0.0 78.4 jit_solution(11719111443973459508)
XLA Ops:
  0.0 76.3 %blocks.1 = f32[16,64,180]{2,1,0:T(8,128)} custom-call(bf16[16,64,180]{2,1,0:T(8,128)(2,1)} %refs_0_.1, bf16[3,180,540]{2,1,0:T(8,128)(2,1)} %refs_1_.1, bf16[3,180,180]{2,1,0:T(8,128)(2,1)} %refs_2_.1, bf16[3,9,60,180]{3,2,1,0:T(8,128)(2,1)} %bitcast.4, bf16[3,9,60,180]{3,2,1,0:T(8,128)(2,1)} %refs_4_.1, bf16[3,6,180]{2,1,0:T(8,128)(2,1)} %bitcast.7, ...), custom_call_target="tpu_custom_call" | custom-call | tf_op jit(solution)/shard_map/blocks/pallas_call | solution.py:671
  76.3 2.1 %convert_element_type.3 = bf16[16,64,180]{2,1,0:T(8,128)(2,1)} convert(f32[16,64,180]{2,1,0:T(8,128)} %blocks.1) | non-fusion elementwise | flops 184320 | bytes 1105920 | tf_op jit(solution)/shard_map/convert_element_type | solution.py:681

commit v4 on v3

--- a/solution.py
+++ b/solution.py
@@ -130,10 +130,10 @@
         tok, qkv_h, proj_h, sq_h, ex_h, gd_h, gu_h, m1_h, m2_h, oqkv_h, oproj_h, out,
         rqkv, rproj, rsq, rex, rgd, rgu, rm1, rm2, roqkv, roproj,
         wqkv, wp, w1, w2, gd, gu, m1, m2, tmp, pn, pm, pd,
-        st, un, ue, ua, qs, ks, vs, qe, ke, ve, oe, att, ex, h32, arf,
-    ) = refs[:49]
-    bufs = refs[49 : 49 + 6 * len(GROUPS)]
-    wsem, hs, hr, asend, arecv, ready = refs[49 + 6 * len(GROUPS) :]
+        st, uf, un, ue, ua, qs, ks, vs, qe, ke, ve, oe, att, ex, h32, arf,
+    ) = refs[:50]
+    bufs = refs[50 : 50 + 6 * len(GROUPS)]
+    wsem, hs, hr, asend, arecv, ready = refs[50 + 6 * len(GROUPS) :]
     row_s, row_r, col_s, col_r, cor_s, cor_r = (bufs[i :: 6] for i in range(6))
     row = lax.axis_index("row")
     col = lax.axis_index("col")
@@ -239,28 +239,30 @@
         ]
         return [
             remote(s, d, hs.at[g, i], hr.at[g, i], p)
-            for i, (s, d, p) in enumerate(plan)
-            if i in which
+            for i in which
+            for s, d, p in plan[i : i + 1]
         ]
 
     def send_rows(g):
         d0, n, _ = GROUPS[g]
-        top = un[d0 : d0 + n].astype(F32)
-        low = un[H - d0 - n : H - d0].astype(F32)
+        top = uf[d0 : d0 + n]
+        low = uf[H - d0 - n : H - d0]
         pack(top, row_s[g].at[0])
         pack(low, row_s[g].at[1])
         pack(fold(top[:, 0:8]), cor_s[g].at[0])
         pack(fold(top[:, W - 8 : W]), cor_s[g].at[1])
         pack(fold(low[:, 0:8]), cor_s[g].at[2])
         pack(fold(low[:, W - 8 : W]), cor_s[g].at[3])
-        low_half, top_half = copies_of(g, (1, 6, 7)), copies_of(g, (0, 4, 5))
-        start(low_half)
-        start(top_half)
+        low_half, top_half = copies_of(g, (6, 7, 1)), copies_of(g, (4, 5, 0))
+        if g == 2:
+            start(low_half)
+        else:
+            start(low_half[:2] + top_half[:2] + low_half[2:] + top_half[2:])
         return low_half, top_half
 
     def send_sides(g):
-        pack(fold(un[:, 0:16].astype(F32)[:, 0:8]), col_s[g].at[0])
-        pack(fold(un[:, W - 16 : W].astype(F32)[:, 8:16]), col_s[g].at[1])
+        pack(fold(uf[:, 0:8]), col_s[g].at[0])
+        pack(fold(uf[:, W - 8 : W]), col_s[g].at[1])
         sides = copies_of(g, (2, 3))
         start(sides)
         return sides
@@ -298,14 +300,12 @@
             masked[8:24, 0:16] = jnp.concatenate([lside * yes_left, first], axis=1).astype(BF16)
             masked[8:24, 64:80] = jnp.concatenate([last, rside * yes_right], axis=1).astype(BF16)
 
-    def normalize(k, y, rows):
-        u = layer_norm(y)
-        un[rows] = u.astype(BF16)
-        inner = u[:, 8:56].astype(BF16)
-        at = pl.ds(rows.start + 8, rows.size)
-        ue[at, 16:64] = inner
+    def settle(k):
+        un[...] = uf[...].astype(BF16)
+        inner = uf[:, 8:56].astype(BF16)
+        ue[8:24, 16:64] = inner
         if k == 1:
-            ua[at, 16:64] = inner
+            ua[8:24, 16:64] = inner
 
     def project(k, which, x):
         r, c, _ = x.shape
@@ -408,38 +408,52 @@
         for w in range(4):
             far = cross_part(w, (slice(4, 8), slice(24, 28)))
             o = merge_parts(tuple(ref[w] for ref in (pn, pm, pd)), far)
-            oe[:, w * WIN : (w + 1) * WIN] = o.reshape(WIN, WIN, L)
-        o = oe[:, 0:W].reshape(H * W, L)
-        att[:, 0:W] = dot(o, wp[k]).reshape(H, W, L)
-
-
-    def conv_in(k):
-        chunk = 9
-        hrow = iota((chunk, E, 1), 0)
-        hcol = iota((chunk, E, 1), 1)
+            cols = slice(w * WIN, (w + 1) * WIN)
+            x = st[:, cols].reshape(WIN * WIN, L) + dot(o, wp[k])
+            u = layer_norm(x).astype(BF16)
+            h = gelu(dot(u, m1[k])).astype(BF16)
+            y = x + dot(h, m2[k])
+            out[:, cols] = y.reshape(WIN, WIN, L)[:, :, :C].astype(out.dtype)
+
+
+    def conv_in(k, spans):
+        count = sum(n for _, n in spans)
+        hcol = iota((count, E, 1), 1)
         lane = iota((1, 1, 128), 2)
         low = jnp.where(col == 0, 8, 0)
         high = jnp.where(col == COLS - 1, 72, E)
-        rlow = jnp.where(row == 0, 1, 0)
-        rhigh = jnp.where(row == ROWS - 1, 17, 18)
-
-        def step(i, carry):
-            acc = None
-            for a in range(3):
-                x = ue[pl.ds(6 + a + i * chunk, chunk)].reshape(chunk * E, L)
-                y = dot(x, w1[k, a])
-                acc = y if acc is None else acc + y
-            r = acc.reshape(chunk, E, L)
-            first, second = r[:, :, :128], r[:, :, 128:]
-            s = pltpu.roll(first, 1, 1) + pltpu.roll(first, 64, 2) + pltpu.roll(second, E - 1, 1)
-            g = gelu(s)
-            at = hrow + i * chunk
-            ok = (at >= rlow) & (at < rhigh) & (hcol >= low) & (hcol < high) & (lane < 60)
-            h32[pl.ds(i * chunk, chunk)] = jnp.where(ok, g, 0.0).astype(BF16).astype(F32)
-            return carry
-
-        for i in range(18 // chunk):
-            step(i, 0)
+        at = iota((count, E, 1), 0) + spans[0][0]
+        if len(spans) > 1:
+            at = at + jnp.where(at >= spans[0][0] + spans[0][1], spans[1][0] - spans[0][1] - spans[0][0], 0)
+        acc = None
+        for a in range(3):
+            x = jnp.concatenate([ue[6 + a + s : 6 + a + s + n] for s, n in spans], axis=0)
+            y = dot(x.reshape(count * E, L), w1[k, a])
+            acc = y if acc is None else acc + y
+        r = acc.reshape(count, E, L)
+        first, second = r[:, :, :128], r[:, :, 128:]
+        s = pltpu.roll(first, 1, 1) + pltpu.roll(first, 64, 2) + pltpu.roll(second, E - 1, 1)
+        ok = (hcol >= low) & (hcol < high) & (lane < 60)
+        if len(spans) > 1:
+            rlow = jnp.where(row == 0, 1, 0)
+            rhigh = jnp.where(row == ROWS - 1, 17, 18)
+            ok = ok & (at >= rlow) & (at < rhigh)
+        g = jnp.where(ok, gelu(s), 0.0).astype(BF16).astype(F32)
+        done = 0
+        for s, n in spans:
+            h32[s : s + n] = g[done : done + n]
+            done += n
+
+    def conv_first(k, g, sides, rows, also=None):
+        whole = ua if k == 1 else None
+        finish(sides)
+        receive_sides(g, ue, whole)
+        conv_in(k, ((2, 14),))
+        if also is not None:
+            also()
+        finish(rows[0] + rows[1])
+        receive_rows(g, ue, whole)
+        conv_in(k, ((0, 2), (16, 2)))
 
     def conv_out(k):
         chunk = 8
@@ -519,42 +533,41 @@
         z = jnp.sum(gu[k] * squeezed, axis=0, keepdims=True)
         return 1.0 / (1.0 + jnp.exp(-z))
 
-    def feed_forward(k, scale, offset, spans):
+    def feed_forward(k, scale, offset, pieces):
         parts = []
-        for at, n in spans:
-            rows = slice(at, at + n)
-            x = st[rows] + att[rows, offset : offset + W]
+        for r, n, c, m in pieces:
+            x = st[r : r + n, c : c + m] + att[r : r + n, offset + c : offset + c + m]
             if scale is not None:
-                x = x + ex[rows] * scale.reshape(1, 1, L)
-            parts.append(x)
+                x = x + ex[r : r + n, c : c + m] * scale.reshape(1, 1, L)
+            parts.append(x.reshape(n * m, L))
         x = jnp.concatenate(parts, axis=0)
-        u = layer_norm(x).astype(BF16).reshape(8 * W, L)
+        u = layer_norm(x).astype(BF16)
         h = gelu(dot(u, m1[k])).astype(BF16)
-        y = x + dot(h, m2[k]).reshape(8, W, L)
+        y = x + dot(h, m2[k])
+        v = layer_norm(y)
         done = 0
-        for at, n in spans:
-            part = y[done : done + n]
-            done += n
-            if k < 3:
-                st[at : at + n] = part
-                normalize(k + 1, part, pl.ds(at, n))
-            else:
-                out[at : at + n] = part[:, :, :C].astype(out.dtype)
+        for r, n, c, m in pieces:
+            span = slice(done, done + n * m)
+            done += n * m
+            st[r : r + n, c : c + m] = y[span].reshape(n, m, L)
+            uf[r : r + n, c : c + m] = v[span].reshape(n, m, L)
 
     def block_end(k, scale, offset, g):
-        feed_forward(k, scale, offset, ((0, 4), (12, 4)))
-        rows = send_rows(g) if k < 3 else None
-        feed_forward(k, scale, offset, ((4, 8),))
-        sides = send_sides(g) if k < 3 else None
+        n = GROUPS[g][1]
+        mid = H - 2 * n
+        feed_forward(k, scale, offset, ((0, n, 0, W), (H - n, n, 0, W), (n, mid, 0, 8), (n, mid, W - 8, 8)))
+        sides, rows = send_sides(g), send_rows(g)
+        feed_forward(k, scale, offset, ((n, mid, 8, W - 16),))
+        settle(k + 1)
         return rows, sides
 
     st[...] = jnp.zeros_like(st)
     st[:, :, :C] = tok[...].astype(F32)
 
-    for i in range(2):
-        normalize(0, st[8 * i : 8 * i + 8], pl.ds(8 * i, 8))
+    uf[...] = layer_norm(st[...])
     pl.semaphore_wait(barrier, len(peers))
-    rows, sides = send_rows(0), send_sides(0)
+    sides, rows = send_sides(0), send_rows(0)
+    settle(0)
     for d in range(1, COLS):
         pl.semaphore_signal(ready, inc=1, device_id=peer(0, d), device_id_type=MESH)
     finish(loads)
@@ -564,30 +577,23 @@
     prepare_mlp(0)
     prepare_attention(1)
     prepare_conv(1)
-    finish(sides + rows[0] + rows[1])
-    receive_sides(0, ue, None)
-    receive_rows(0, ue, None)
-    conv_in(0)
+    prepare_mlp(1)
+    conv_first(0, 0, sides, rows)
     part = expanded_sum(0)
     pl.semaphore_wait(ready, COLS - 1)
     spread(0, part)
     conv_out(0)
     lax.fori_loop(0, 4, plain_window(0), 0)
-    prepare_mlp(1)
     prepare_attention(2)
     prepare_conv(2)
-    prepare_mlp(2)
     rows, sides = block_end(0, gate(0), 0, 1)
 
     more = send_rows(2)
     project_inner(1, ua, ((0, qe, 8), (1, ke, 0), (2, ve, 0)))
-    finish(sides)
-    receive_sides(1, ue, ua)
-    project_sides(1, ua, ((0, qe, 8), (1, ke, 0), (2, ve, 0)))
-    finish(rows[0] + rows[1])
-    receive_rows(1, ue, ua)
-    conv_in(1)
+    prepare_mlp(2)
+    conv_first(1, 1, sides, rows, lambda: project_sides(1, ua, ((0, qe, 8), (1, ke, 0), (2, ve, 0))))
     spread(1, expanded_sum(1))
+    start(more[1])
     conv_out(1)
     finish(more[0])
     receive_rows(2, None, ua, (1,))
@@ -602,10 +608,7 @@
     project_plain(2, (qs, ks, vs))
     prepare_attention(3)
     prepare_mlp(3)
-    finish(sides + rows[0] + rows[1])
-    receive_sides(3, ue, None)
-    receive_rows(3, ue, None)
-    conv_in(2)
+    conv_first(2, 3, sides, rows)
     spread(2, expanded_sum(2))
     conv_out(2)
     lax.fori_loop(0, 4, plain_window(2), 0)
@@ -622,7 +625,6 @@
     receive_rows(4, ue, None)
     project_rows(3, ue, 4)
     cross_far(3)
-    block_end(3, None, 0, None)
 
 
 def local(tok, qkv, proj, squeeze, expand, down, up_, mlp_in, mlp_out, oqkv, oproj):
@@ -646,6 +648,7 @@
         pltpu.VMEM((4, WIN * WIN, L), F32),
         pltpu.VMEM((4, WIN * WIN, L), F32),
         pltpu.VMEM((4, WIN * WIN, L), F32),
+        pltpu.VMEM((H, W, L), F32),
         pltpu.VMEM((H, W, L), F32),
         pltpu.VMEM((H, W, L), BF16),
         pltpu.VMEM((32, E, L), BF16),
@@ -670,7 +673,7 @@
     scratch += [dma((3,)), dma((3,)), pltpu.SemaphoreType.REGULAR]
     return pl.pallas_call(
         kernel,
-        out_shape=jax.ShapeDtypeStruct((H, W, C), F32),
+        out_shape=jax.ShapeDtypeStruct((H, W, C), BF16),
         in_specs=[vmem] + [hbm] * 10,
         out_specs=vmem,
         scratch_shapes=scratch,
@@ -678,7 +681,7 @@
             collective_id=0, has_side_effects=True, vmem_limit_bytes=60 * 1024 * 1024
         ),
         name="blocks",
-    )(*args).astype(BF16)
+    )(*args)
 
 
 def solution(mesh):

time: 78.6 us -> 73.2 us (0.931); the launches traced: 78.4 us -> 72 us
  Pallas kernels: 76.3 us -> 70.1 us
  other arithmetic: 2.09 us -> 0 us
  local copies, waits for them, and re-layouts: 0 us -> 1.88 us
    pallas_call x1, Pallas kernels: 76.3 us -> 70.1 us  [local(): pl.pallas_call(kernel, out_shape=jax.ShapeDtypeStruct((H, W, C), BF16), i...]
    convert_element_type x1 -> x0, other arithmetic: 2.09 us -> none  [local(): return pl.pallas_call(kernel, out_shape=jax.ShapeDtypeStruct((H, W, C), F...]
    unnamed x0 -> x1, local copies, waits for them, and re-layouts: none -> 1.88 us
where the time goes in v4:
time: 73.2 us; the launch traced here: 72 us
  Pallas kernels  70.1 us (96%)
  local copies, waits for them, and re-layouts  1.88 us (3%)
    pallas_call x1, Pallas kernels, local(): pl.pallas_call(kernel, out_shape=jax.ShapeDtypeStruct((H, W, C), BF16), i...  70.1 us
    unnamed x1, local copies, waits for them, and re-layouts  1.88 us

profile of v4, /device:TPU:0, one launch (start us, length us, event | category | flops | bytes accessed | tf_op | source)
XLA Modules:
  0.0 72.0 jit_solution(12701001792387183047)
XLA Ops:
  0.0 70.1 %blocks.1 = bf16[16,64,180]{2,1,0:T(8,128)(2,1)} custom-call(bf16[16,64,180]{2,1,0:T(8,128)(2,1)} %refs_0_.1, bf16[3,180,540]{2,1,0:T(8,128)(2,1)} %refs_1_.1, bf16[3,180,180]{2,1,0:T(8,128)(2,1)} %refs_2_.1, bf16[3,9,60,180]{3,2,1,0:T(8,128)(2,1)} %bitcast.4, bf16[3,9,60,180]{3,2,1,0:T(8,128)(2,1)} %refs_4_.1, bf16[3,6,180]{2,1,0:T(8,128)(2,1)} %bitcast.7, ...), custom_call_target="tpu_custom_call" | custom-call | tf_op jit(solution)/shard_map/blocks/pallas_call | solution.py:674
  70.1 1.9 %copy.13 = bf16[16,64,180]{2,1,0:T(8,128)(2,1)} copy(bf16[16,64,180]{2,1,0:T(8,128)(2,1)} %blocks.1) | data formatting | bytes 737280

commit v5 on v4

--- a/solution.py
+++ b/solution.py
@@ -584,8 +584,6 @@
     spread(0, part)
     conv_out(0)
     lax.fori_loop(0, 4, plain_window(0), 0)
-    prepare_attention(2)
-    prepare_conv(2)
     rows, sides = block_end(0, gate(0), 0, 1)
 
     more = send_rows(2)
@@ -599,6 +597,8 @@
     receive_rows(2, None, ua, (1,))
     project_rows(1, ua, 8, (1,))
     shifted_windows(1, 0)
+    prepare_attention(2)
+    prepare_conv(2)
     finish(more[1])
     receive_rows(2, None, ua, (0,))
     project_rows(1, ua, 8, (0,))

time: 73.2 us -> 73.4 us (level)
  no operation moved by 1% of the time
where the time goes in v5:
time: 73.4 us; the launch traced here: 72.2 us
  Pallas kernels  70.3 us (96%)
  local copies, waits for them, and re-layouts  1.88 us (3%)
    pallas_call x1, Pallas kernels, local(): pl.pallas_call(kernel, out_shape=jax.ShapeDtypeStruct((H, W, C), BF16), i...  70.3 us
    unnamed x1, local copies, waits for them, and re-layouts  1.88 us

profile of v5, /device:TPU:0, one launch (start us, length us, event | category | flops | bytes accessed | tf_op | source)
XLA Modules:
  0.0 72.2 jit_solution(1576599350535284723)
XLA Ops:
  0.0 70.3 %blocks.1 = bf16[16,64,180]{2,1,0:T(8,128)(2,1)} custom-call(bf16[16,64,180]{2,1,0:T(8,128)(2,1)} %refs_0_.1, bf16[3,180,540]{2,1,0:T(8,128)(2,1)} %refs_1_.1, bf16[3,180,180]{2,1,0:T(8,128)(2,1)} %refs_2_.1, bf16[3,9,60,180]{3,2,1,0:T(8,128)(2,1)} %bitcast.4, bf16[3,9,60,180]{3,2,1,0:T(8,128)(2,1)} %refs_4_.1, bf16[3,6,180]{2,1,0:T(8,128)(2,1)} %bitcast.7, ...), custom_call_target="tpu_custom_call" | custom-call | tf_op jit(solution)/shard_map/blocks/pallas_call | solution.py:674
  70.3 1.9 %copy.13 = bf16[16,64,180]{2,1,0:T(8,128)(2,1)} copy(bf16[16,64,180]{2,1,0:T(8,128)(2,1)} %blocks.1) | data formatting | bytes 737280
